TPU v7x, 256 devices: a whole 4x4x8 slice. The times are simulated.
256 devices in a mesh: cell: 32 (over x, z), mem: 8 (over y, core).
Axes of the slice: x: 4, y: 4, z: 8, core: 2. Of those that a mesh axis runs over, the one named last changes fastest.
Arguments:
- logperm: float32 [128, 64, 64, 256], P('mem', 'cell'), may hold values from -4 to 4
- source: float32 [64, 64, 256], P('cell'), may hold values from -6 to 6
- obs_cells: int32 [4096], replicated, may hold values from 0 to 1048575
- obs_values: float32 [4096], replicated, may hold values from -2 to 2
- obs_prec: float32 [4096], replicated, may hold values from 0.1 to 10
Outputs:
- pressure: float32 [128, 64, 64, 256], P('mem', 'cell')
- analysis: float32 [128, 64, 64, 256], P('mem', 'cell')
All inputs are finite; a program needn't handle non-finite values. Where the computation divides by a largest or mean magnitude, that divisor is 1e-20 or more.
Results may differ from a plain program's by a relative error of at most 0.00015.
Values sent between devices are 32-bit elements; how exact they have to be, the bound alone decides.
No kernel may reach another device: no remote copies, remote signals or barrier semaphores. Data moves between devices by JAX's collectives and lax.ppermute only.
A program may use at most 128 MiB of HBM per device.

v0:
```python
import jax
import jax.numpy as jnp
from jax import lax
from jax.experimental import pallas as pl
from jax.experimental.pallas import tpu as pltpu
from jax.sharding import Mesh
from jax.sharding import PartitionSpec as P

M = 128
NOBS = 4096
NS_STEPS = 10
CPRESS = 0.05
HIGH = lax.Precision.HIGHEST
F32 = jnp.float32

NX, NZ, NMEM = 4, 8, 8
LAY = 2
MEM = M // NMEM
SUB = MEM // NZ
DEPTH = NZ * LAY
HALO = 4
FULL = DEPTH + 2 * HALO
GROUP = 4
ROOM = FULL + 6
NY, NW = 64, 256
HALVES = NW // 128
ROWS_OF = NY // NMEM
CHUNK = 1280
BLOCK_BITS = 18

VM = pl.BlockSpec(memory_space=pltpu.VMEM)
SM = pl.BlockSpec(memory_space=pltpu.SMEM)
ANY = pl.BlockSpec(memory_space=pl.ANY)
HBM = pl.BlockSpec(memory_space=pltpu.HBM)


def shape(*dims):
    return jax.ShapeDtypeStruct(dims, F32)


def call(kernel, outs, ins, specs, out_specs, scratch, flops, moved):
    return pl.pallas_call(
        kernel,
        out_shape=outs,
        in_specs=specs,
        out_specs=out_specs,
        scratch_shapes=scratch,
        cost_estimate=pl.CostEstimate(flops=flops, bytes_accessed=moved, transcendentals=0),
        compiler_params=pltpu.CompilerParams(vmem_limit_bytes=48 * 2**20),
    )(*ins)


def roots_kernel(where, *refs):
    parts, (h_ref, first_ref, last_ref, buffer, sems) = refs[:NZ], refs[NZ:]
    copies = [pltpu.make_async_copy(parts[d], buffer.at[d], sems.at[d]) for d in range(NZ)]
    for copy in copies:
        copy.start()
    for d in range(NZ):
        copies[d].wait()
        slab = (where[0] + d) & (NZ - 1)
        for m in range(SUB):
            for a in range(LAY):
                h_ref[m, slab * LAY + a] = jnp.exp(0.5 * buffer[d, m, a])
    first_ref[...] = h_ref[:, 0:HALO]
    last_ref[...] = h_ref[:, DEPTH - HALO : DEPTH]


TILES = [(i, half) for i in range(NY // 8) for half in range(NW // 128)]


def tile(i, half):
    return pl.ds(8 * i, 8), pl.ds(128 * half, 128)


def lane_sums(q, j, band, sums):
    value = q[pl.ds(j, GROUP)].reshape(GROUP * NY, NW)
    high = value.astype(jnp.bfloat16)
    low = (value - high.astype(F32)).astype(jnp.bfloat16)
    both = jnp.dot(jnp.concatenate([high, low], axis=0), band[...], preferred_element_type=F32)
    both = both[: GROUP * NY] + both[GROUP * NY :]
    sums[pl.ds(j, GROUP)] = both.reshape(GROUP, NY, NW)


def near_sums(q, sums, j):
    row = lax.broadcasted_iota(jnp.int32, (8, 128), 0)
    middle = {t: q[(j, *tile(*t))] for t in TILES}
    below = {t: pltpu.roll(middle[t], 1, 0) for t in TILES}
    above = {t: pltpu.roll(middle[t], 7, 0) for t in TILES}
    total = {}
    for i, half in TILES:
        t = (i, half)
        side = jnp.where(row == 0, below.get((i - 1, half), 0.0), below[t])
        side = side + jnp.where(row == 7, above.get((i + 1, half), 0.0), above[t])
        side = side + sums[(j, *tile(*t))]
        total[t] = side + (q[(j - 1, *tile(*t))] + q[(j + 1, *tile(*t))])
    return middle, total


def over_layers(q, band, sums, first, groups, step):
    lane_sums(q, first, band, sums)

    @pl.loop(0, groups)
    def _(c):
        j = first + c * GROUP
        for k in range(GROUP):
            step(j + k)
        lane_sums(q, j + GROUP, band, sums)


def gather_all(where, spots, lanes, press, found, copies):
    out = copies.at[0]
    out[...] = jnp.zeros_like(out)
    low, high = where[1] // 128, (where[2] + 127) // 128
    lane = lax.broadcasted_iota(jnp.int32, (1, 128), 1)
    flat = [press.at[m].reshape(HALVES * DEPTH * NY, 128) for m in range(SUB)]

    @pl.loop(low, high)
    def _(k):
        def one(o, carry):
            at = k * 128 + o
            spot, wanted = spots[at], lanes[at]
            for m in range(SUB):
                row = flat[m][pl.ds(spot, 1), :]
                found[m, pl.ds(o, 1), :] = jnp.where(lane == wanted, row, 0.0)
            return carry

        lax.fori_loop(0, 128, one, 0, unroll=16)
        for m in range(SUB):
            out[k, m : m + 1, :] = jnp.sum(found[m].T, axis=0, keepdims=True)

    for copy in range(1, NZ):
        copies[copy] = out[...]


def sweeps_kernel(where, spots, lanes, h_ref, hl_ref, hr_ref, s_ref, *refs):
    out, pred_ref, h, qs, qw, qb, qc, rest, weight, sums, band, press, found, sems = refs

    def results(m):
        copies = []
        for slab in range(NZ):
            for half in range(HALVES):
                done = press.at[m, half, pl.ds(slab * LAY, LAY)]
                place = out.at[slab, m, :, :, pl.ds(128 * half, 128)]
                copies.append(pltpu.make_async_copy(done, place, sems.at[m, half, slab]))
        return copies

    row = lax.broadcasted_iota(jnp.int32, (NW, NW), 0)
    column = lax.broadcasted_iota(jnp.int32, (NW, NW), 1)
    band[...] = jnp.where(jnp.abs(row - column) == 1, 1.0, 0.0).astype(jnp.bfloat16)
    h[0] = jnp.zeros((NY, NW), F32)
    h[FULL + 1 : ROOM] = jnp.zeros((ROOM - FULL - 1, NY, NW), F32)

    @pl.loop(0, SUB)
    def _(m):
        h[1 : 1 + HALO] = hl_ref[m]
        h[1 + HALO : 1 + HALO + DEPTH] = h_ref[m]
        h[1 + HALO + DEPTH : 1 + FULL] = hr_ref[m]

        def prepare(j):
            root, near = near_sums(h, sums, j)
            for i, half in TILES:
                t, spot = (i, half), (j, *tile(i, half))
                inverse = 1.0 / (CPRESS + root[t] * near[t])
                start = s_ref[i, j - 1, :, pl.ds(128 * half, 128)] * inverse
                slope = root[t] * inverse
                rest[spot] = start
                weight[spot] = slope
                qs[spot] = root[t] * start
                qw[spot] = root[t] * slope

        def sweep_to(new, old):
            def step(j):
                _, near = near_sums(old, sums, j)
                for t in TILES:
                    spot = (j, *tile(*t))
                    new[spot] = qs[spot] + qw[spot] * near[t]

            return step

        def last(j):
            _, near = near_sums(qc, sums, j)
            for i, half in TILES:
                spot = (j, *tile(i, half))
                value = rest[spot] + weight[spot] * near[i, half]
                press[m, half, j - HALO - 1, pl.ds(8 * i, 8), :] = value

        over_layers(h, band, sums, 2, 6, prepare)
        over_layers(qs, band, sums, 3, 5, sweep_to(qb, qs))
        over_layers(qb, band, sums, 4, 5, sweep_to(qc, qb))
        over_layers(qc, band, sums, 5, 4, last)

        for copy in results(m):
            copy.start()

    gather_all(where, spots, lanes, press, found, pred_ref)

    @pl.loop(0, SUB)
    def _(m):
        for copy in results(m):
            copy.wait()


def more_kernel(where, spots, lanes, parts, pred_ref, press, found):
    for slab in range(NZ):
        for m in range(SUB):
            for half in range(HALVES):
                lanes_of = pl.ds(128 * half, 128)
                press[m, half, slab * LAY : slab * LAY + LAY] = parts[slab, m, :, :, lanes_of]
    gather_all(where, spots, lanes, press, found, pred_ref)


def gram_kernel(mem, *refs):
    parts, (prec_ref, value_ref, out_ref, preds) = refs[:NMEM], refs[NMEM:]
    for e in range(NMEM):
        preds[group_at(mem[0], e)] = parts[e][...]
    pred = jnp.concatenate([preds[:, k].reshape(M, 128) for k in range(CHUNK // 128)], axis=1)
    prec = prec_ref[...]
    mean = jnp.sum(pred, axis=0, keepdims=True) * (1.0 / M)
    anomaly = pred - mean
    contract = (((1,), (1,)), ((), ()))
    out_ref[0:M] = lax.dot_general(
        anomaly * prec, anomaly, contract, precision=HIGH, preferred_element_type=F32
    )
    misfit = jnp.broadcast_to(prec * (value_ref[...] - mean), (8, CHUNK))
    out_ref[M : M + 8] = lax.dot_general(
        misfit, anomaly, contract, precision=HIGH, preferred_element_type=F32
    )


def dot(a, b):
    return jnp.dot(a, b, precision=HIGH, preferred_element_type=F32)


PIECES = 8
ROWS = LAY * NY // PIECES


BLOCKS = [(0, 0), (1, 0), (3, 0), (2, 0), (2, MEM // 2)]


def analysis_kernel(where, g0, g1, g2, g3, *refs):
    states, (out, buffer, done, turned, sems, out_sems) = refs[: 2 * len(BLOCKS)], refs[2 * len(BLOCKS) :]

    def place(k, half):
        layer, first = k // (NY // ROWS), pl.multiple_of(k % (NY // ROWS) * ROWS, ROWS)
        return (slice(None), layer, pl.ds(first, ROWS), pl.ds(half * 128, 128))

    def pieces(k, half):
        y, core = where[3] // 2, where[3] & 1
        copies = []
        for n, source in enumerate(states):
            step, first = BLOCKS[n % len(BLOCKS)]
            group = ((y + step) & 3) * 2 + (core if n < len(BLOCKS) else 1 - core)
            rows = pl.ds(group * MEM + first, source.shape[0])
            there = buffer.at[k, half, rows]
            copies.append(pltpu.make_async_copy(source.at[place(k, half)], there, sems.at[k, half, n]))
        return copies

    def result(k, half):
        return pltpu.make_async_copy(
            done.at[k, half], out.at[place(k, half)], out_sems.at[k, half]
        )

    @pl.loop(0, PIECES)
    def _(k):
        for half in range(HALVES):
            for copy in pieces(k, half):
                copy.start()

    sums = (g0[...] + g1[...]) + (g2[...] + g3[...])
    row = lax.broadcasted_iota(jnp.int32, (M, M), 0)
    column = lax.broadcasted_iota(jnp.int32, (M, M), 1)
    identity = jnp.where(row == column, 1.0, 0.0).astype(F32)
    scaled = identity + sums[0:M] / (M - 1)
    bound = jnp.max(jnp.sum(jnp.abs(scaled), axis=1, keepdims=True), axis=0, keepdims=True)
    root = scaled / bound
    inv_root = 1.5 * identity - 0.5 * root
    root = dot(root, inv_root)
    for step in range(1, NS_STEPS):
        factor = 1.5 * identity - 0.5 * dot(inv_root, root)
        if step < NS_STEPS - 1:
            root = dot(root, factor)
        inv_root = dot(factor, inv_root)
    contract = (((1,), (1,)), ((), ()))
    shift = sums[M : M + 8]
    for _ in range(2):
        shift = lax.dot_general(shift, inv_root, contract, precision=HIGH, preferred_element_type=F32)
    shift = shift[0:1] / bound / (M - 1)
    turned[...] = inv_root.T / jnp.sqrt(bound) + shift
    mine = turned[pl.ds(pl.multiple_of(where[3] * MEM, MEM), MEM), :]
    mine = mine + (1.0 - jnp.sum(mine, axis=1, keepdims=True)) * (1.0 / M)
    high = mine.astype(jnp.bfloat16)
    low = (mine - high.astype(F32)).astype(jnp.bfloat16)
    left = jnp.concatenate(
        [
            jnp.concatenate([high, high], axis=1),
            jnp.concatenate([low, jnp.zeros_like(low)], axis=1),
        ],
        axis=0,
    )

    @pl.loop(0, PIECES)
    def _(k):
        for half in range(HALVES):
            for copy in pieces(k, half):
                copy.wait()
        given = [buffer.at[k, half].reshape(M * ROWS, 128) for half in range(HALVES)]
        taken = [done.at[k, half].reshape(MEM * ROWS, 128) for half in range(HALVES)]
        for r in range(ROWS):
            state = jnp.concatenate([g[pl.ds(r, M, stride=ROWS), :] for g in given], axis=1)
            upper = state.astype(jnp.bfloat16)
            lower = (state - upper.astype(F32)).astype(jnp.bfloat16)
            both = jnp.dot(
                left, jnp.concatenate([upper, lower], axis=0), preferred_element_type=F32
            )
            both = both[:MEM] + both[MEM:]
            for half in range(HALVES):
                taken[half][pl.ds(r, MEM, stride=ROWS), :] = both[:, half * 128 : half * 128 + 128]
        for half in range(HALVES):
            result(k, half).start()

    for k in range(PIECES):
        for half in range(HALVES):
            result(k, half).wait()


BIG = SUB * DEPTH * NY * NW
PARTS = shape(NZ, SUB, LAY, NY, NW)
PRED = shape(NZ, CHUNK // 128, SUB, 128)
PRESSED = pltpu.VMEM((SUB, HALVES, DEPTH, NY, 128), F32)
FOUND = pltpu.VMEM((SUB, 128, 128), F32)


def sweep(*ins):
    return call(
        sweeps_kernel,
        [PARTS, PRED],
        ins,
        [SM] * 3 + [VM] * 4,
        [HBM, VM],
        [pltpu.VMEM((ROOM, NY, NW), F32)] * 8
        + [pltpu.VMEM((NW, NW), jnp.bfloat16), PRESSED, FOUND]
        + [pltpu.SemaphoreType.DMA((SUB, HALVES, NZ))],
        64 * BIG,
        16 * BIG,
    )


def analyse(where, sums, states):
    return call(
        analysis_kernel,
        shape(MEM, LAY, NY, NW),
        [where, *sums, *states],
        [SM] + [VM] * NX + [HBM] * (2 * len(BLOCKS)),
        ANY,
        [
            pltpu.VMEM((PIECES, HALVES, M, ROWS, 128), F32),
            pltpu.VMEM((PIECES, HALVES, MEM, ROWS, 128), F32),
            pltpu.VMEM((M, M), F32),
            pltpu.SemaphoreType.DMA((PIECES, HALVES, 2 * len(BLOCKS))),
            pltpu.SemaphoreType.DMA((PIECES, HALVES)),
        ],
        2 * M * MEM * LAY * NY * NW,
        4 * M * LAY * NY * NW,
    )


def shift_from(array, axis, size, by):
    return lax.ppermute(array, axis, [((i + by) % size, i) for i in range(size)])


def exchange(copies, axis):
    return lax.all_to_all(copies, axis, 0, 0, tiled=True)


def strip_kernel(mem, source, out, sems):
    copies = []
    for slab in range(NZ):
        rows = source.at[:, pl.ds(pl.multiple_of(mem[0] * ROWS_OF, ROWS_OF), ROWS_OF)]
        copies.append(pltpu.make_async_copy(rows, out.at[slab], sems.at[slab]))
    for copy in copies:
        copy.start()
    for copy in copies:
        copy.wait()


def strips_kernel(strips, out):
    for copy in range(NMEM):
        for slab in range(NZ):
            out[copy, LAY * slab : LAY * slab + LAY] = strips[slab]


def preds_kernel(parts, out):
    for g in range(NZ):
        for m in range(SUB):
            for k in range(CHUNK // 128):
                row = g * SUB + m
                out[k, row : row + 1, :] = parts[g, k, m : m + 1, :]


def group_at(mem, e):
    return (((mem // 2 + e // 2) & (NMEM // 2 - 1)) * 2) + ((mem & 1) ^ (e & 1))


def round_mem(array):
    parts = [array]
    for e in range(1, NMEM):
        pairs = [(group_at(i, e), i) for i in range(NMEM)]
        parts.append(lax.ppermute(array, ("y", "core"), pairs))
    return parts


def to_mem(kernel, parts, dims):
    copies = call(kernel, shape(NMEM, *dims), [parts], [VM], VM, [], 2**20, 2**20)
    return exchange(copies, ("y", "core"))


def body(logperm, source, obs_cells, obs_values, obs_prec):
    x, z, mem = lax.axis_index("x"), lax.axis_index("z"), lax.axis_index(("y", "core"))

    def swapped(array):
        return lax.ppermute(array, "core", [(0, 1), (1, 0)])

    half = MEM // 2
    after, before = shift_from(logperm, "y", 4, 1), shift_from(logperm, "y", 4, 3)
    far_a, far_b = shift_from(after[:half], "y", 4, 1), shift_from(before[half:], "y", 4, 3)
    others = [swapped(array) for array in (logperm, after, before)]
    others += [swapped(array) for array in (far_a, far_b)]
    states = [logperm, after, before, far_a, far_b, *others]

    strip = call(
        strip_kernel,
        shape(NZ, LAY, ROWS_OF, NW),
        [jnp.reshape(mem, (1,)).astype(jnp.int32), source],
        [SM, VM],
        HBM,
        [pltpu.SemaphoreType.DMA((NZ,))],
        2**20,
        2**20,
    )
    strips = exchange(strip, "z")

    def members_of(group):
        start = ((group & (NZ - 1)) * SUB, 0, 0, 0)
        sizes = (SUB, LAY, NY, NW)
        return lax.dynamic_slice(logperm, start, sizes, allow_negative_indices=False)

    parts = [members_of(z)] + [None] * (NZ - 1)
    for d in (4, 1, 7, 2, 6, 3, 5):
        parts[d] = shift_from(members_of(z - d), "z", NZ, d)
    sources = to_mem(strips_kernel, strips, (DEPTH, ROWS_OF, NW))

    cells, prec, values = lax.sort((obs_cells, obs_prec, obs_values), num_keys=1)
    block = lax.shift_right_logical(cells, BLOCK_BITS)
    counts = jnp.sum(block[None, :] == jnp.arange(NX)[:, None], axis=1).astype(jnp.int32)
    begin = jnp.sum(jnp.where(jnp.arange(NX) < x, counts, 0))
    count = jnp.sum(jnp.where(jnp.arange(NX) == x, counts, 0))
    most = jnp.max(counts)

    def window(done):
        want = jnp.minimum(begin + done, begin + count)
        first = jnp.minimum(want, NOBS - CHUNK)
        stop = jnp.minimum(want + CHUNK, begin + count)
        where = jnp.stack([z, want - first, jnp.maximum(stop - first, 0), mem]).astype(jnp.int32)

        def cut(array):
            return lax.dynamic_slice(array, (first,), (CHUNK,), allow_negative_indices=False)

        at = cut(cells)
        half = lax.shift_right_logical(at, 7) & (HALVES - 1)
        spots = half * (DEPTH * NY) + (lax.shift_right_logical(at, 8) & (DEPTH * NY - 1))
        place = jnp.arange(CHUNK, dtype=jnp.int32)
        lanes = jnp.where((place >= where[1]) & (place < where[2]), at & 127, -1)
        return where, spots, lanes, cut(prec)[None], cut(values)[None]

    where, spots_0, lanes_0, prec_0, values_0 = window(0)
    edge = shape(SUB, HALO, NY, NW)
    h, first, last = call(
        roots_kernel,
        [shape(SUB, DEPTH, NY, NW), edge, edge],
        [jnp.reshape(z, (1,)).astype(jnp.int32), *parts],
        [SM] + [HBM] * NZ,
        [VM] * 3,
        [pltpu.VMEM((NZ, SUB, LAY, NY, NW), F32), pltpu.SemaphoreType.DMA((NZ,))],
        4 * BIG,
        12 * BIG,
    )
    up = [(i, i + 1) for i in range(NX - 1)]
    down = [(i + 1, i) for i in range(NX - 1)]
    h_left, h_right = lax.ppermute(last, "x", up), lax.ppermute(first, "x", down)
    s_left = lax.ppermute(sources[:, DEPTH - HALO :], "x", up)
    s_right = lax.ppermute(sources[:, :HALO], "x", down)

    spare = jnp.zeros((NMEM, 2, ROWS_OF, NW), F32)
    sources = jnp.concatenate([s_left, sources, s_right, spare], axis=1)
    sent, pred = sweep(where, spots_0, lanes_0, h, h_left, h_right, sources)

    def group_preds(parts):
        dims = (CHUNK // 128, MEM, 128)
        return call(preds_kernel, shape(*dims), [parts], [VM], VM, [], 2**20, 2**20)

    def gram_of(first, parts, prec_cut, value_cut):
        return call(
            gram_kernel,
            shape(M + 8, M),
            [jnp.reshape(first, (1,)).astype(jnp.int32), *parts, prec_cut, value_cut],
            [SM] + [VM] * (NMEM + 2),
            VM,
            [pltpu.VMEM((NMEM, CHUNK // 128, MEM, 128), F32)],
            2 * M * M * CHUNK,
            4 * M * CHUNK,
        )

    def more(carry):
        done, total = carry
        where_n, spots_n, lanes_n, prec_n, values_n = window(done)
        pred_n = call(
            more_kernel,
            PRED,
            [where_n, spots_n, lanes_n, sent],
            [SM] * 3 + [VM],
            VM,
            [PRESSED, FOUND],
            BIG,
            8 * BIG,
        )
        group = group_preds(lax.all_gather(pred_n[0], "z"))
        groups = lax.all_gather(group, ("y", "core"))
        split = [groups[g] for g in range(NMEM)]
        return done + CHUNK, total + gram_of(jnp.int32(0), split, prec_n, values_n)

    gathered = exchange(pred, "z")
    groups = round_mem(group_preds(gathered))
    total = gram_of(mem, groups, prec_0, values_0)
    pressure = exchange(sent.reshape(MEM, LAY, NY, NW), "z")
    _, total = lax.while_loop(lambda c: c[0] < most, more, (jnp.int32(CHUNK), total))
    others = [shift_from(total, "x", NX, d) for d in range(1, NX)]

    analysis = analyse(where, [total, *others], states)
    return pressure, analysis


def solution(mesh):
    fine = Mesh(mesh.devices.reshape(NX, NZ, NMEM // 2, 2), ("x", "z", "y", "core"))
    cell, mem = ("x", "z"), ("y", "core")
    return jax.shard_map(
        body,
        mesh=fine,
        in_specs=(P(mem, cell, None, None), P(cell, None, None), P(), P(), P()),
        out_specs=(P(mem, cell, None, None), P(mem, cell, None, None)),
        check_vma=False,
    )
```

profile of v0, /device:TPU:64, one launch (start us, length us, event | category | flops | bytes accessed | tf_op | source)
XLA Modules:
  0.0 255.6 jit_solution(9428266193414642549)
XLA Ops:
  1.7 14.2 %all_to_all.20.strips = f32[8,2,8,256]{3,2,1,0:T(8,128)S(1)} all-to-all(f32[8,2,8,256]{3,2,1,0:T(8,128)S(1)} %shard_map.69), channel_id=1, replica_groups=mesh['x'=4,'z'=8,'y'=4,'core'=2] {'z'}, dimensions={0} | all-to-all | bytes 262144 | tf_op jit(solution)/shard_map/all_to_all | solution.py:373
  17.0 4.5 %all-to-all-start.1 = ((f32[8,16,8,256]{3,2,1,0:T(8,128)}), f32[8,16,8,256]{3,2,1,0:T(8,128)}, u32[]{:S(2)}, u32[]{:S(2)}) async-start(f32[8,16,8,256]{3,2,1,0:T(8,128)} %shard_map.70), calls=%async_computation.1 | async-start | bytes 2097152 | tf_op jit(solution)/shard_map/all_to_all | solution.py:373
  25.2 4.6 %collective-permute-start.4 = (f32[2,2,64,256]{3,2,1,0:T(8,128)}, f32[2,2,64,256]{3,2,1,0:T(8,128)S(1)}, u32[]{:S(2)}, u32[]{:S(2)}) collective-permute-start(f32[2,2,64,256]{3,2,1,0:T(8,128)} %get-tuple-element.189), channel_id=1, source_target_pairs={{40,0},{48,8},{56,16},{0,24},{8,32},{16,40},{24,48},{32,56},{41,1}... | collective-permute-start | bytes 786440 | tf_op jit(solution)/shard_map/ppermute | solution.py:369
  30.3 4.3 %collective-permute-start.2 = (f32[2,2,64,256]{3,2,1,0:T(8,128)}, f32[2,2,64,256]{3,2,1,0:T(8,128)S(1)}, u32[]{:S(2)}, u32[]{:S(2)}) collective-permute-start(f32[2,2,64,256]{3,2,1,0:T(8,128)} %get-tuple-element.191), channel_id=1, source_target_pairs={{24,0},{32,8},{40,16},{48,24},{56,32},{0,40},{8,48},{16,56},{25,1}... | collective-permute-start | bytes 786440 | tf_op jit(solution)/shard_map/ppermute | solution.py:369
  34.7 5.9 %sort.31 = (s32[4096]{0:T(1024)S(1)}, f32[4096]{0:T(1024)S(1)}, f32[4096]{0:T(1024)S(1)}, s32[4096]{0:T(1024)}) sort(s32[4096]{0:T(1024)S(1)} %copy-done.8, f32[4096]{0:T(1024)S(1)} %copy-done.9, f32[4096]{0:T(1024)S(1)} %copy-done.10, s32[4096]{0:T(1024)S(1)} %iota.26), dimensions={0}, to_apply=%region_0.0 | sort | flops 49152 | bytes 131072 | tf_op jit(solution)/shard_map/sort | solution.py:453
  42.1 10.1 %collective-permute-start = (f32[2,2,64,256]{3,2,1,0:T(8,128)}, f32[2,2,64,256]{3,2,1,0:T(8,128)S(1)}, u32[]{:S(2)}, u32[]{:S(2)}) collective-permute-start(f32[2,2,64,256]{3,2,1,0:T(8,128)} %get-tuple-element.193), channel_id=1, source_target_pairs={{8,0},{16,8},{24,16},{32,24},{40,32},{48,40},{56,48},{0,56},{9,1},... | collective-permute-start | bytes 786440 | tf_op jit(solution)/shard_map/ppermute | solution.py:369
  52.3 22.2 %collective-permute-done.4.refs_5_ = f32[2,2,64,256]{3,2,1,0:T(8,128)S(1)} collective-permute-done((f32[2,2,64,256]{3,2,1,0:T(8,128)}, f32[2,2,64,256]{3,2,1,0:T(8,128)S(1)}, u32[]{:S(2)}, u32[]{:S(2)}) %collective-permute-start.4) | collective-permute-done | bytes 262176 | tf_op jit(solution)/shard_map/ppermute | solution.py:369
  75.3 1.8 collective-permute-done.refs_1_
  78.0 1.7 shard_map.68
  79.7 3.4 %collective-permute-start.7 = (f32[2,4,64,256]{3,2,1,0:T(8,128)}, f32[2,4,64,256]{3,2,1,0:T(8,128)S(1)}, u32[]{:S(2)}, u32[]{:S(2)}) collective-permute-start(f32[2,4,64,256]{3,2,1,0:T(8,128)} %get-tuple-element.145), channel_id=1, source_target_pairs={{0,64},{64,128},{128,192},{1,65},{65,129},{129,193},{2,66},{66,130... | collective-permute-start | bytes 1572872 | tf_op jit(solution)/shard_map/ppermute | solution.py:490
  84.4 1.8 fusion.6
  86.2 5.3 %collective-permute-start.9 = (f32[8,4,8,256]{3,2,1,0:T(8,128)}, f32[8,4,8,256]{3,2,1,0:T(8,128)}, u32[]{:S(2)}, u32[]{:S(2)}) collective-permute-start(f32[8,4,8,256]{3,2,1,0:T(8,128)} %get-tuple-element.195), channel_id=1, source_target_pairs={{0,64},{64,128},{128,192},{1,65},{65,129},{129,193},{2,66},{66,130... | collective-permute-start | bytes 786440 | tf_op jit(solution)/shard_map/ppermute | solution.py:491
  95.6 3.8 %collective-permute-done.9 = f32[8,4,8,256]{3,2,1,0:T(8,128)} collective-permute-done((f32[8,4,8,256]{3,2,1,0:T(8,128)}, f32[8,4,8,256]{3,2,1,0:T(8,128)}, u32[]{:S(2)}, u32[]{:S(2)}) %collective-permute-start.9) | collective-permute-done | bytes 262176 | tf_op jit(solution)/shard_map/ppermute | solution.py:491
  99.4 4.1 %collective-permute-done.10 = f32[8,4,8,256]{3,2,1,0:T(8,128)} collective-permute-done((f32[8,4,8,256]{3,2,1,0:T(8,128)S(1)}, f32[8,4,8,256]{3,2,1,0:T(8,128)}, u32[]{:S(2)}, u32[]{:S(2)}) %collective-permute-start.10) | collective-permute-done | bytes 262176 | tf_op jit(solution)/shard_map/ppermute | solution.py:492
  103.6 1.5 maximum_maximum_fusion.s_ref
  105.2 18.0 %shard_map.71 = (f32[8,2,2,64,256]{4,3,2,1,0:T(8,128)}, f32[8,10,2,128]{3,2,1,0:T(2,128)S(1)}) custom-call(s32[4]{0:T(128)S(1)} %pad_add_fusion.1.where, s32[1280]{0:T(1024)S(1)} %get-tuple-element.198.spots, s32[1280]{0:T(1024)S(1)} %get-tuple-element.197.lanes, f32[2,16,64,256]{3,2,1,0:T(8,128)S(1)} %get-tuple-element.144.h_ref, ...), custom_call_target="tpu_custom_call" | custom-call | flops 33554432 | bytes 8388608 | tf_op jit(solution)/shard_map/pallas_call | solution.py:42
  123.2 13.9 %all_to_all.21.parts = f32[8,10,2,128]{3,2,1,0:T(2,128)S(1)} all-to-all(f32[8,10,2,128]{3,2,1,0:T(2,128)S(1)} %get-tuple-element.148), channel_id=1, replica_groups=mesh['x'=4,'z'=8,'y'=4,'core'=2] {'z'}, dimensions={0} | all-to-all | bytes 163840 | tf_op jit(solution)/shard_map/all_to_all | solution.py:373
  137.2 1.7 collective-permute-start.16
  138.9 2.4 collective-permute-start.15
  141.4 1.9 collective-permute-start.14
  143.5 1.6 collective-permute-start.12
  145.5 6.8 %all-to-all-start.2 = ((f32[16,2,64,256]{3,2,1,0:T(8,128)}), f32[16,2,64,256]{3,2,1,0:T(8,128)}, u32[]{:S(2)}, u32[]{:S(2)}) async-start(f32[16,2,64,256]{3,2,1,0:T(8,128)} %bitcast.17), calls=%async_computation.2 | async-start | bytes 4194304 | tf_op jit(solution)/shard_map/all_to_all | solution.py:373
  152.3 1.6 collective-permute-start.21
  156.2 1.9 collective-permute-start.20
  159.1 2.5 collective-permute-start.18
  161.6 38.6 %collective-permute-done.21.refs_1_ = f32[16,2,64,256]{3,2,1,0:T(8,128)} collective-permute-done((f32[16,2,64,256]{3,2,1,0:T(8,128)}, f32[16,2,64,256]{3,2,1,0:T(8,128)}, u32[]{:S(2)}, u32[]{:S(2)}) %collective-permute-start.21) | collective-permute-done | bytes 2097184 | tf_op jit(solution)/shard_map/ppermute | solution.py:369
  202.5 1.7 collective-permute-start.23
  206.4 20.8 %collective-permute-done.23.refs_3_ = f32[8,2,64,256]{3,2,1,0:T(8,128)S(1)} collective-permute-done((f32[8,2,64,256]{3,2,1,0:T(8,128)S(1)}, f32[8,2,64,256]{3,2,1,0:T(8,128)S(1)}, u32[]{:S(2)}, u32[]{:S(2)}) %collective-permute-start.23) | collective-permute-done | bytes 1048608 | tf_op jit(solution)/shard_map/ppermute | solution.py:369
  227.2 4.8 %collective-permute-done.24.refs_4_ = f32[8,2,64,256]{3,2,1,0:T(8,128)S(1)} collective-permute-done((f32[8,2,64,256]{3,2,1,0:T(8,128)S(1)}, f32[8,2,64,256]{3,2,1,0:T(8,128)S(1)}, u32[]{:S(2)}, u32[]{:S(2)}) %collective-permute-start.24) | collective-permute-done | bytes 1048608 | tf_op jit(solution)/shard_map/ppermute | solution.py:369
  232.1 2.6 %collective-permute-done.29.refs_9_ = f32[8,2,64,256]{3,2,1,0:T(8,128)S(1)} collective-permute-done((f32[8,2,64,256]{3,2,1,0:T(8,128)S(1)}, f32[8,2,64,256]{3,2,1,0:T(8,128)S(1)}, u32[]{:S(2)}, u32[]{:S(2)}) %collective-permute-start.29) | collective-permute-done | bytes 1048608 | tf_op jit(solution)/shard_map/ppermute | solution.py:422
  236.0 16.4 %shard_map.74 = f32[16,2,64,256]{3,2,1,0:T(8,128)} custom-call(s32[4]{0:T(128)S(1)} %pad_add_fusion.1.where, f32[136,128]{1,0:T(8,128)S(1)} %get-tuple-element.151.g0, f32[136,128]{1,0:T(8,128)S(1)} %collective-permute-done.18.g1, f32[136,128]{1,0:T(8,128)S(1)} %collective-permute-done.19.g2, f32[136,128]{1,0:T(8,128)S(1)} %collective-permute-done.20.g3, ...), custom_call_target="tpu_custom_call" | custom-call | flops 134217728 | bytes 16777216 | tf_op jit(solution)/shard_map/pallas_call | solution.py:42
  252.4 3.1 %copy.14 = f32[16,2,64,256]{3,2,1,0:T(8,128)} copy(f32[16,2,64,256]{3,2,1,0:T(8,128)} %all-to-all-done.2) | data formatting | bytes 4194304
  (83 shorter events, 22.8 us)
Async XLA Ops:
  17.0 67.4 %all-to-all-start.1 = ((f32[8,16,8,256]{3,2,1,0:T(8,128)}), f32[8,16,8,256]{3,2,1,0:T(8,128)}, u32[]{:S(2)}, u32[]{:S(2)}) async-start(f32[8,16,8,256]{3,2,1,0:T(8,128)} %shard_map.70), calls=%async_computation.1 | async-start | bytes 2097152 | tf_op jit(solution)/shard_map/all_to_all | solution.py:373
  22.8 17.8 %collective-permute-start.6 = (f32[2,2,64,256]{3,2,1,0:T(8,128)}, f32[2,2,64,256]{3,2,1,0:T(8,128)S(1)}, u32[]{:S(2)}, u32[]{:S(2)}) collective-permute-start(f32[2,2,64,256]{3,2,1,0:T(8,128)} %get-tuple-element.187), channel_id=1, source_target_pairs={{56,0},{0,8},{8,16},{16,24},{24,32},{32,40},{40,48},{48,56},{57,1}... | collective-permute-start | bytes 786440 | tf_op jit(solution)/shard_map/ppermute | solution.py:369
  23.9 18.2 %collective-permute-start.5 = (f32[2,2,64,256]{3,2,1,0:T(8,128)}, f32[2,2,64,256]{3,2,1,0:T(8,128)S(1)}, u32[]{:S(2)}, u32[]{:S(2)}) collective-permute-start(f32[2,2,64,256]{3,2,1,0:T(8,128)} %get-tuple-element.188), channel_id=1, source_target_pairs={{48,0},{56,8},{0,16},{8,24},{16,32},{24,40},{32,48},{40,56},{49,1}... | collective-permute-start | bytes 786440 | tf_op jit(solution)/shard_map/ppermute | solution.py:369
  25.2 49.4 %collective-permute-start.4 = (f32[2,2,64,256]{3,2,1,0:T(8,128)}, f32[2,2,64,256]{3,2,1,0:T(8,128)S(1)}, u32[]{:S(2)}, u32[]{:S(2)}) collective-permute-start(f32[2,2,64,256]{3,2,1,0:T(8,128)} %get-tuple-element.189), channel_id=1, source_target_pairs={{40,0},{48,8},{56,16},{0,24},{8,32},{16,40},{24,48},{32,56},{41,1}... | collective-permute-start | bytes 786440 | tf_op jit(solution)/shard_map/ppermute | solution.py:369
  29.8 44.7 %collective-permute-start.3 = (f32[2,2,64,256]{3,2,1,0:T(8,128)}, f32[2,2,64,256]{3,2,1,0:T(8,128)S(1)}, u32[]{:S(2)}, u32[]{:S(2)}) collective-permute-start(f32[2,2,64,256]{3,2,1,0:T(8,128)} %get-tuple-element.190), channel_id=1, source_target_pairs={{32,0},{40,8},{48,16},{56,24},{0,32},{8,40},{16,48},{24,56},{33,1}... | collective-permute-start | bytes 786440 | tf_op jit(solution)/shard_map/ppermute | solution.py:369
  30.3 44.2 %collective-permute-start.2 = (f32[2,2,64,256]{3,2,1,0:T(8,128)}, f32[2,2,64,256]{3,2,1,0:T(8,128)S(1)}, u32[]{:S(2)}, u32[]{:S(2)}) collective-permute-start(f32[2,2,64,256]{3,2,1,0:T(8,128)} %get-tuple-element.191), channel_id=1, source_target_pairs={{24,0},{32,8},{40,16},{48,24},{56,32},{0,40},{8,48},{16,56},{25,1}... | collective-permute-start | bytes 786440 | tf_op jit(solution)/shard_map/ppermute | solution.py:369
  40.6 34.7 %collective-permute-start.1 = (f32[2,2,64,256]{3,2,1,0:T(8,128)}, f32[2,2,64,256]{3,2,1,0:T(8,128)S(1)}, u32[]{:S(2)}, u32[]{:S(2)}) collective-permute-start(f32[2,2,64,256]{3,2,1,0:T(8,128)} %get-tuple-element.192), channel_id=1, source_target_pairs={{16,0},{24,8},{32,16},{40,24},{48,32},{56,40},{0,48},{8,56},{17,1}... | collective-permute-start | bytes 786440 | tf_op jit(solution)/shard_map/ppermute | solution.py:369
  42.1 34.9 %collective-permute-start = (f32[2,2,64,256]{3,2,1,0:T(8,128)}, f32[2,2,64,256]{3,2,1,0:T(8,128)S(1)}, u32[]{:S(2)}, u32[]{:S(2)}) collective-permute-start(f32[2,2,64,256]{3,2,1,0:T(8,128)} %get-tuple-element.193), channel_id=1, source_target_pairs={{8,0},{16,8},{24,16},{32,24},{40,32},{48,40},{56,48},{0,56},{9,1},... | collective-permute-start | bytes 786440 | tf_op jit(solution)/shard_map/ppermute | solution.py:369
  79.7 25.5 %collective-permute-start.7 = (f32[2,4,64,256]{3,2,1,0:T(8,128)}, f32[2,4,64,256]{3,2,1,0:T(8,128)S(1)}, u32[]{:S(2)}, u32[]{:S(2)}) collective-permute-start(f32[2,4,64,256]{3,2,1,0:T(8,128)} %get-tuple-element.145), channel_id=1, source_target_pairs={{0,64},{64,128},{128,192},{1,65},{65,129},{129,193},{2,66},{66,130... | collective-permute-start | bytes 1572872 | tf_op jit(solution)/shard_map/ppermute | solution.py:490
  83.1 22.1 %collective-permute-start.8 = (f32[2,4,64,256]{3,2,1,0:T(8,128)}, f32[2,4,64,256]{3,2,1,0:T(8,128)S(1)}, u32[]{:S(2)}, u32[]{:S(2)}) collective-permute-start(f32[2,4,64,256]{3,2,1,0:T(8,128)} %get-tuple-element.146), channel_id=1, source_target_pairs={{64,0},{128,64},{192,128},{65,1},{129,65},{193,129},{66,2},{130,66... | collective-permute-start | bytes 1572872 | tf_op jit(solution)/shard_map/ppermute | solution.py:490
  86.2 13.3 %collective-permute-start.9 = (f32[8,4,8,256]{3,2,1,0:T(8,128)}, f32[8,4,8,256]{3,2,1,0:T(8,128)}, u32[]{:S(2)}, u32[]{:S(2)}) collective-permute-start(f32[8,4,8,256]{3,2,1,0:T(8,128)} %get-tuple-element.195), channel_id=1, source_target_pairs={{0,64},{64,128},{128,192},{1,65},{65,129},{129,193},{2,66},{66,130... | collective-permute-start | bytes 786440 | tf_op jit(solution)/shard_map/ppermute | solution.py:491
  91.4 12.2 %collective-permute-start.10 = (f32[8,4,8,256]{3,2,1,0:T(8,128)S(1)}, f32[8,4,8,256]{3,2,1,0:T(8,128)}, u32[]{:S(2)}, u32[]{:S(2)}) collective-permute-start(f32[8,4,8,256]{3,2,1,0:T(8,128)S(1)} %get-tuple-element.196), channel_id=1, source_target_pairs={{64,0},{128,64},{192,128},{65,1},{129,65},{193,129},{66,2},{130,66... | collective-permute-start | bytes 786440 | tf_op jit(solution)/shard_map/ppermute | solution.py:492
  137.1 6.4 %collective-permute-start.17 = (f32[10,16,128]{2,1,0:T(8,128)S(1)}, f32[10,16,128]{2,1,0:T(8,128)S(1)}, u32[]{:S(2)}, u32[]{:S(2)}) collective-permute-start(f32[10,16,128]{2,1,0:T(8,128)S(1)} %shard_map.72.refs_0_), channel_id=1, source_target_pairs={{7,0},{6,1},{1,2},{0,3},{3,4},{2,5},{5,6},{4,7},{15,8},{14,9},{9,1... | collective-permute-start | bytes 245768 | tf_op jit(solution)/shard_map/ppermute | solution.py:409
  137.2 7.9 %collective-permute-start.16 = (f32[10,16,128]{2,1,0:T(8,128)S(1)}, f32[10,16,128]{2,1,0:T(8,128)S(1)}, u32[]{:S(2)}, u32[]{:S(2)}) collective-permute-start(f32[10,16,128]{2,1,0:T(8,128)S(1)} %shard_map.72.refs_0_), channel_id=1, source_target_pairs={{6,0},{7,1},{0,2},{1,3},{2,4},{3,5},{4,6},{5,7},{14,8},{15,9},{8,1... | collective-permute-start | bytes 245768 | tf_op jit(solution)/shard_map/ppermute | solution.py:409
  138.9 13.4 %collective-permute-start.15 = (f32[10,16,128]{2,1,0:T(8,128)S(1)}, f32[10,16,128]{2,1,0:T(8,128)S(1)}, u32[]{:S(2)}, u32[]{:S(2)}) collective-permute-start(f32[10,16,128]{2,1,0:T(8,128)S(1)} %shard_map.72.refs_0_), channel_id=1, source_target_pairs={{5,0},{4,1},{7,2},{6,3},{1,4},{0,5},{3,6},{2,7},{13,8},{12,9},{15,... | collective-permute-start | bytes 245768 | tf_op jit(solution)/shard_map/ppermute | solution.py:409
  141.4 12.6 %collective-permute-start.14 = (f32[10,16,128]{2,1,0:T(8,128)S(1)}, f32[10,16,128]{2,1,0:T(8,128)S(1)}, u32[]{:S(2)}, u32[]{:S(2)}) collective-permute-start(f32[10,16,128]{2,1,0:T(8,128)S(1)} %shard_map.72.refs_0_), channel_id=1, source_target_pairs={{4,0},{5,1},{6,2},{7,3},{0,4},{1,5},{2,6},{3,7},{12,8},{13,9},{14,... | collective-permute-start | bytes 245768 | tf_op jit(solution)/shard_map/ppermute | solution.py:409
  143.3 11.1 %collective-permute-start.13 = (f32[10,16,128]{2,1,0:T(8,128)S(1)}, f32[10,16,128]{2,1,0:T(8,128)S(1)}, u32[]{:S(2)}, u32[]{:S(2)}) collective-permute-start(f32[10,16,128]{2,1,0:T(8,128)S(1)} %shard_map.72.refs_0_), channel_id=1, source_target_pairs={{3,0},{2,1},{5,2},{4,3},{7,4},{6,5},{1,6},{0,7},{11,8},{10,9},{13,... | collective-permute-start | bytes 245768 | tf_op jit(solution)/shard_map/ppermute | solution.py:409
  143.5 10.8 %collective-permute-start.12 = (f32[10,16,128]{2,1,0:T(8,128)S(1)}, f32[10,16,128]{2,1,0:T(8,128)S(1)}, u32[]{:S(2)}, u32[]{:S(2)}) collective-permute-start(f32[10,16,128]{2,1,0:T(8,128)S(1)} %shard_map.72.refs_0_), channel_id=1, source_target_pairs={{2,0},{3,1},{4,2},{5,3},{6,4},{7,5},{0,6},{1,7},{10,8},{11,9},{12,... | collective-permute-start | bytes 245768 | tf_op jit(solution)/shard_map/ppermute | solution.py:409
  145.2 9.2 %collective-permute-start.11 = (f32[10,16,128]{2,1,0:T(8,128)S(1)}, f32[10,16,128]{2,1,0:T(8,128)S(1)}, u32[]{:S(2)}, u32[]{:S(2)}) collective-permute-start(f32[10,16,128]{2,1,0:T(8,128)S(1)} %shard_map.72.refs_0_), channel_id=1, source_target_pairs={{1,0},{0,1},{3,2},{2,3},{5,4},{4,5},{7,6},{6,7},{9,8},{8,9},{11,10... | collective-permute-start | bytes 245768 | tf_op jit(solution)/shard_map/ppermute | solution.py:409
  145.5 107.0 %all-to-all-start.2 = ((f32[16,2,64,256]{3,2,1,0:T(8,128)}), f32[16,2,64,256]{3,2,1,0:T(8,128)}, u32[]{:S(2)}, u32[]{:S(2)}) async-start(f32[16,2,64,256]{3,2,1,0:T(8,128)} %bitcast.17), calls=%async_computation.2 | async-start | bytes 4194304 | tf_op jit(solution)/shard_map/all_to_all | solution.py:373
  152.3 47.9 %collective-permute-start.21 = (f32[16,2,64,256]{3,2,1,0:T(8,128)}, f32[16,2,64,256]{3,2,1,0:T(8,128)}, u32[]{:S(2)}, u32[]{:S(2)}) collective-permute-start(f32[16,2,64,256]{3,2,1,0:T(8,128)} %refs_0_.1), channel_id=1, source_target_pairs={{2,0},{4,2},{6,4},{0,6},{3,1},{5,3},{7,5},{1,7},{10,8},{12,10},{14... | collective-permute-start | bytes 6291464 | tf_op jit(solution)/shard_map/ppermute | solution.py:369
  153.9 48.5 %collective-permute-start.22 = (f32[16,2,64,256]{3,2,1,0:T(8,128)}, f32[16,2,64,256]{3,2,1,0:T(8,128)}, u32[]{:S(2)}, u32[]{:S(2)}) collective-permute-start(f32[16,2,64,256]{3,2,1,0:T(8,128)} %refs_0_.1), channel_id=1, source_target_pairs={{6,0},{0,2},{2,4},{4,6},{7,1},{1,3},{3,5},{5,7},{14,8},{8,10},{10,... | collective-permute-start | bytes 6291464 | tf_op jit(solution)/shard_map/ppermute | solution.py:369
  156.2 49.2 %collective-permute-start.20 = (f32[136,128]{1,0:T(8,128)S(1)}, f32[136,128]{1,0:T(8,128)S(1)}, u32[]{:S(2)}, u32[]{:S(2)}) collective-permute-start(f32[136,128]{1,0:T(8,128)S(1)} %get-tuple-element.151.g0), channel_id=1, source_target_pairs={{192,0},{0,64},{64,128},{128,192},{193,1},{1,65},{65,129},{129,193... | collective-permute-start | bytes 208904 | tf_op jit(solution)/shard_map/ppermute | solution.py:369
  158.1 47.8 %collective-permute-start.19 = (f32[136,128]{1,0:T(8,128)S(1)}, f32[136,128]{1,0:T(8,128)S(1)}, u32[]{:S(2)}, u32[]{:S(2)}) collective-permute-start(f32[136,128]{1,0:T(8,128)S(1)} %get-tuple-element.151.g0), channel_id=1, source_target_pairs={{128,0},{192,64},{0,128},{64,192},{129,1},{193,65},{1,129},{65,193... | collective-permute-start | bytes 208904 | tf_op jit(solution)/shard_map/ppermute | solution.py:369
  159.1 46.8 %collective-permute-start.18 = (f32[136,128]{1,0:T(8,128)S(1)}, f32[136,128]{1,0:T(8,128)S(1)}, u32[]{:S(2)}, u32[]{:S(2)}) collective-permute-start(f32[136,128]{1,0:T(8,128)S(1)} %get-tuple-element.151.g0), channel_id=1, source_target_pairs={{64,0},{128,64},{192,128},{0,192},{65,1},{129,65},{193,129},{1,193... | collective-permute-start | bytes 208904 | tf_op jit(solution)/shard_map/ppermute | solution.py:369
  200.3 31.8 %collective-permute-start.25 = (f32[16,2,64,256]{3,2,1,0:T(8,128)}, f32[16,2,64,256]{3,2,1,0:T(8,128)S(1)}, u32[]{:S(2)}, u32[]{:S(2)}) collective-permute-start(f32[16,2,64,256]{3,2,1,0:T(8,128)} %refs_0_.1), channel_id=1, source_target_pairs={{0,1},{1,0},{2,3},{3,2},{4,5},{5,4},{6,7},{7,6},{8,9},{9,8},{10,11... | collective-permute-start | bytes 6291464 | tf_op jit(solution)/shard_map/ppermute | solution.py:422
  202.5 24.8 %collective-permute-start.23 = (f32[8,2,64,256]{3,2,1,0:T(8,128)S(1)}, f32[8,2,64,256]{3,2,1,0:T(8,128)S(1)}, u32[]{:S(2)}, u32[]{:S(2)}) collective-permute-start(f32[8,2,64,256]{3,2,1,0:T(8,128)S(1)} %slice.80), channel_id=1, source_target_pairs={{2,0},{4,2},{6,4},{0,6},{3,1},{5,3},{7,5},{1,7},{10,8},{12,10},{14... | collective-permute-start | bytes 3145736 | tf_op jit(solution)/shard_map/ppermute | solution.py:369
  205.4 26.6 %collective-permute-start.24 = (f32[8,2,64,256]{3,2,1,0:T(8,128)S(1)}, f32[8,2,64,256]{3,2,1,0:T(8,128)S(1)}, u32[]{:S(2)}, u32[]{:S(2)}) collective-permute-start(f32[8,2,64,256]{3,2,1,0:T(8,128)S(1)} %slice.81), channel_id=1, source_target_pairs={{6,0},{0,2},{2,4},{4,6},{7,1},{1,3},{3,5},{5,7},{14,8},{8,10},{10,... | collective-permute-start | bytes 3145736 | tf_op jit(solution)/shard_map/ppermute | solution.py:369
  205.9 26.2 %collective-permute-start.26 = (f32[16,2,64,256]{3,2,1,0:T(8,128)}, f32[16,2,64,256]{3,2,1,0:T(8,128)S(1)}, u32[]{:S(2)}, u32[]{:S(2)}) collective-permute-start(f32[16,2,64,256]{3,2,1,0:T(8,128)} %collective-permute-done.21.refs_1_), channel_id=1, source_target_pairs={{0,1},{1,0},{2,3},{3,2},{4,5},{5,4},{6,7},{7,6},{8,9},{9,8},{10,11... | collective-permute-start | bytes 6291464 | tf_op jit(solution)/shard_map/ppermute | solution.py:422
  205.9 28.8 %collective-permute-start.27 = (f32[16,2,64,256]{3,2,1,0:T(8,128)}, f32[16,2,64,256]{3,2,1,0:T(8,128)S(1)}, u32[]{:S(2)}, u32[]{:S(2)}) collective-permute-start(f32[16,2,64,256]{3,2,1,0:T(8,128)} %collective-permute-done.22.refs_2_), channel_id=1, source_target_pairs={{0,1},{1,0},{2,3},{3,2},{4,5},{5,4},{6,7},{7,6},{8,9},{9,8},{10,11... | collective-permute-start | bytes 6291464 | tf_op jit(solution)/shard_map/ppermute | solution.py:422
  227.2 4.8 %collective-permute-start.28 = (f32[8,2,64,256]{3,2,1,0:T(8,128)S(1)}, f32[8,2,64,256]{3,2,1,0:T(8,128)S(1)}, u32[]{:S(2)}, u32[]{:S(2)}) collective-permute-start(f32[8,2,64,256]{3,2,1,0:T(8,128)S(1)} %collective-permute-done.23.refs_3_), channel_id=1, source_target_pairs={{0,1},{1,0},{2,3},{3,2},{4,5},{5,4},{6,7},{7,6},{8,9},{9,8},{10,11... | collective-permute-start | bytes 3145736 | tf_op jit(solution)/shard_map/ppermute | solution.py:422
  232.0 2.7 %collective-permute-start.29 = (f32[8,2,64,256]{3,2,1,0:T(8,128)S(1)}, f32[8,2,64,256]{3,2,1,0:T(8,128)S(1)}, u32[]{:S(2)}, u32[]{:S(2)}) collective-permute-start(f32[8,2,64,256]{3,2,1,0:T(8,128)S(1)} %collective-permute-done.24.refs_4_), channel_id=1, source_target_pairs={{0,1},{1,0},{2,3},{3,2},{4,5},{5,4},{6,7},{7,6},{8,9},{9,8},{10,11... | collective-permute-start | bytes 3145736 | tf_op jit(solution)/shard_map/ppermute | solution.py:422
  (11 other events, 78.8 us)
where the time goes:
time: 258 us; the launch traced here: 256 us
  waiting for transfers between devices  99.8 us (39%)
  starting transfers between devices  64.2 us (25%)
  Pallas kernels  38.5 us (15%)
  blocking collectives  28.2 us (11%)
  local copies, waits for them, and re-layouts  12.9 us (5%)
  other arithmetic  8.52 us (3%)
  between operations  2.87 us (1%)
    ppermute x14, waiting for transfers between devices, shift_from(): lax.ppermute(array, axis, [((i + by) % size, i) for i in range(size)])  89.2 us
    pallas_call x7, Pallas kernels, call(): pl.pallas_call(kernel, out_shape=outs, in_specs=specs, out_specs=out_spec...  38.5 us
    ppermute x14, starting transfers between devices, shift_from(): lax.ppermute(array, axis, [((i + by) % size, i) for i in range(size)])  33 us
    all_to_all x2, blocking collectives, exchange(): return lax.all_to_all(copies, axis, 0, 0, tiled=True)  28.2 us
    all_to_all x2, starting transfers between devices, exchange(): return lax.all_to_all(copies, axis, 0, 0, tiled=True)  11.3 us
    ppermute x7, starting transfers between devices, round_mem(): parts.append(lax.ppermute(array, ('y', 'core'), pairs))  8.14 us
    unnamed x23, local copies, waits for them, and re-layouts  7.06 us
    sort x1, other arithmetic, body(): lax.sort((obs_cells, obs_prec, obs_values), num_keys=1)  5.94 us
  transfers between devices with their start and end apart: 32, of which 9 were waited for; matrix products, arithmetic and copies ran while one was open for 6% of the time, Pallas kernels for 8%

commit v1 on v0

--- a/solution.py
+++ b/solution.py
@@ -38,7 +38,10 @@
     return jax.ShapeDtypeStruct(dims, F32)
 
 
-def call(kernel, outs, ins, specs, out_specs, scratch, flops, moved):
+LIMITS = {"roots": 16, "sweeps": 32, "analysis": 32, "more": 16}
+
+
+def call(kernel, outs, ins, specs, out_specs, scratch, flops, moved, name):
     return pl.pallas_call(
         kernel,
         out_shape=outs,
@@ -46,23 +49,29 @@
         out_specs=out_specs,
         scratch_shapes=scratch,
         cost_estimate=pl.CostEstimate(flops=flops, bytes_accessed=moved, transcendentals=0),
-        compiler_params=pltpu.CompilerParams(vmem_limit_bytes=48 * 2**20),
+        compiler_params=pltpu.CompilerParams(vmem_limit_bytes=LIMITS.get(name, 8) * 2**20),
     )(*ins)
 
 
 def roots_kernel(where, *refs):
-    parts, (h_ref, first_ref, last_ref, buffer, sems) = refs[:NZ], refs[NZ:]
+    parts, (h_ref, first_ref, last_ref, buffer, h, sems, out_sems) = refs[:NZ], refs[NZ:]
     copies = [pltpu.make_async_copy(parts[d], buffer.at[d], sems.at[d]) for d in range(NZ)]
     for copy in copies:
         copy.start()
+    results = []
     for d in range(NZ):
         copies[d].wait()
         slab = (where[0] + d) & (NZ - 1)
         for m in range(SUB):
             for a in range(LAY):
-                h_ref[m, slab * LAY + a] = jnp.exp(0.5 * buffer[d, m, a])
-    first_ref[...] = h_ref[:, 0:HALO]
-    last_ref[...] = h_ref[:, DEPTH - HALO : DEPTH]
+                h[m, slab * LAY + a] = jnp.exp(0.5 * buffer[d, m, a])
+        layers = pl.ds(slab * LAY, LAY)
+        results.append(pltpu.make_async_copy(h.at[:, layers], h_ref.at[:, layers], out_sems.at[d]))
+        results[-1].start()
+    first_ref[...] = h[:, 0:HALO]
+    last_ref[...] = h[:, DEPTH - HALO : DEPTH]
+    for result in results:
+        result.wait()
 
 
 TILES = [(i, half) for i in range(NY // 8) for half in range(NW // 128)]
@@ -132,8 +141,25 @@
         copies[copy] = out[...]
 
 
-def sweeps_kernel(where, spots, lanes, h_ref, hl_ref, hr_ref, s_ref, *refs):
-    out, pred_ref, h, qs, qw, qb, qc, rest, weight, sums, band, press, found, sems = refs
+def sweeps_kernel(where, spots, lanes, h_ref, hl_ref, hr_ref, s_mid, sl_ref, sr_ref, *refs):
+    out, pred_ref, h_all, s_ref, qs, qw, qb, qc, rest, weight, sums, band, *refs = refs
+    press, found, sems, in_sems, s_sems = refs
+    cuts = [(0, HALO), (HALO, DEPTH), (HALO + DEPTH, HALO)]
+
+    def roots(m):
+        copies = []
+        for n, source in enumerate((hl_ref, h_ref, hr_ref)):
+            first, layers = cuts[n]
+            there = h_all.at[m, pl.ds(1 + first, layers)]
+            copies.append(pltpu.make_async_copy(source.at[m], there, in_sems.at[m, n]))
+        return copies
+
+    strips = []
+    for n, source in enumerate((sl_ref, s_mid, sr_ref)):
+        there = s_ref.at[:, pl.ds(*cuts[n])]
+        strips.append(pltpu.make_async_copy(source, there, s_sems.at[n]))
+    for copy in [*roots(0), *strips, *roots(1)]:
+        copy.start()
 
     def results(m):
         copies = []
@@ -147,14 +173,18 @@
     row = lax.broadcasted_iota(jnp.int32, (NW, NW), 0)
     column = lax.broadcasted_iota(jnp.int32, (NW, NW), 1)
     band[...] = jnp.where(jnp.abs(row - column) == 1, 1.0, 0.0).astype(jnp.bfloat16)
-    h[0] = jnp.zeros((NY, NW), F32)
-    h[FULL + 1 : ROOM] = jnp.zeros((ROOM - FULL - 1, NY, NW), F32)
+    s_ref[:, FULL : FULL + 2] = jnp.zeros((NMEM, 2, ROWS_OF, NW), F32)
+    for m in range(SUB):
+        h_all[m, 0] = jnp.zeros((NY, NW), F32)
+        h_all[m, FULL + 1 : ROOM] = jnp.zeros((ROOM - FULL - 1, NY, NW), F32)
+    for copy in strips:
+        copy.wait()
 
     @pl.loop(0, SUB)
     def _(m):
-        h[1 : 1 + HALO] = hl_ref[m]
-        h[1 + HALO : 1 + HALO + DEPTH] = h_ref[m]
-        h[1 + HALO + DEPTH : 1 + FULL] = hr_ref[m]
+        for copy in roots(m):
+            copy.wait()
+        h = h_all.at[m]
 
         def prepare(j):
             root, near = near_sums(h, sums, j)
@@ -336,13 +366,16 @@
         sweeps_kernel,
         [PARTS, PRED],
         ins,
-        [SM] * 3 + [VM] * 4,
+        [SM] * 3 + [HBM] + [ANY] * 5,
         [HBM, VM],
-        [pltpu.VMEM((ROOM, NY, NW), F32)] * 8
+        [pltpu.VMEM((SUB, ROOM, NY, NW), F32), pltpu.VMEM((NMEM, FULL + 2, ROWS_OF, NW), F32)]
+        + [pltpu.VMEM((ROOM, NY, NW), F32)] * 7
         + [pltpu.VMEM((NW, NW), jnp.bfloat16), PRESSED, FOUND]
-        + [pltpu.SemaphoreType.DMA((SUB, HALVES, NZ))],
+        + [pltpu.SemaphoreType.DMA((SUB, HALVES, NZ))]
+        + [pltpu.SemaphoreType.DMA((SUB, 3)), pltpu.SemaphoreType.DMA((3,))],
         64 * BIG,
         16 * BIG,
+        "sweeps",
     )
 
 
@@ -362,6 +395,7 @@
         ],
         2 * M * MEM * LAY * NY * NW,
         4 * M * LAY * NY * NW,
+        "analysis",
     )
 
 
@@ -410,8 +444,8 @@
     return parts
 
 
-def to_mem(kernel, parts, dims):
-    copies = call(kernel, shape(NMEM, *dims), [parts], [VM], VM, [], 2**20, 2**20)
+def to_mem(kernel, parts, dims, name):
+    copies = call(kernel, shape(NMEM, *dims), [parts], [VM], VM, [], 2**20, 2**20, name)
     return exchange(copies, ("y", "core"))
 
 
@@ -430,13 +464,14 @@
 
     strip = call(
         strip_kernel,
-        shape(NZ, LAY, ROWS_OF, NW),
+        pltpu.HBM((NZ, LAY, ROWS_OF, NW), F32),
         [jnp.reshape(mem, (1,)).astype(jnp.int32), source],
         [SM, VM],
         HBM,
         [pltpu.SemaphoreType.DMA((NZ,))],
         2**20,
         2**20,
+        "strip",
     )
     strips = exchange(strip, "z")
 
@@ -448,7 +483,7 @@
     parts = [members_of(z)] + [None] * (NZ - 1)
     for d in (4, 1, 7, 2, 6, 3, 5):
         parts[d] = shift_from(members_of(z - d), "z", NZ, d)
-    sources = to_mem(strips_kernel, strips, (DEPTH, ROWS_OF, NW))
+    sources = to_mem(strips_kernel, strips, (DEPTH, ROWS_OF, NW), "strips")
 
     cells, prec, values = lax.sort((obs_cells, obs_prec, obs_values), num_keys=1)
     block = lax.shift_right_logical(cells, BLOCK_BITS)
@@ -477,13 +512,19 @@
     edge = shape(SUB, HALO, NY, NW)
     h, first, last = call(
         roots_kernel,
-        [shape(SUB, DEPTH, NY, NW), edge, edge],
+        [pltpu.HBM((SUB, DEPTH, NY, NW), F32), edge, edge],
         [jnp.reshape(z, (1,)).astype(jnp.int32), *parts],
-        [SM] + [HBM] * NZ,
-        [VM] * 3,
-        [pltpu.VMEM((NZ, SUB, LAY, NY, NW), F32), pltpu.SemaphoreType.DMA((NZ,))],
+        [SM] + [ANY] * NZ,
+        [HBM, VM, VM],
+        [
+            pltpu.VMEM((NZ, SUB, LAY, NY, NW), F32),
+            pltpu.VMEM((SUB, DEPTH, NY, NW), F32),
+            pltpu.SemaphoreType.DMA((NZ,)),
+            pltpu.SemaphoreType.DMA((NZ,)),
+        ],
         4 * BIG,
         12 * BIG,
+        "roots",
     )
     up = [(i, i + 1) for i in range(NX - 1)]
     down = [(i + 1, i) for i in range(NX - 1)]
@@ -491,13 +532,11 @@
     s_left = lax.ppermute(sources[:, DEPTH - HALO :], "x", up)
     s_right = lax.ppermute(sources[:, :HALO], "x", down)
 
-    spare = jnp.zeros((NMEM, 2, ROWS_OF, NW), F32)
-    sources = jnp.concatenate([s_left, sources, s_right, spare], axis=1)
-    sent, pred = sweep(where, spots_0, lanes_0, h, h_left, h_right, sources)
+    sent, pred = sweep(where, spots_0, lanes_0, h, h_left, h_right, sources, s_left, s_right)
 
     def group_preds(parts):
         dims = (CHUNK // 128, MEM, 128)
-        return call(preds_kernel, shape(*dims), [parts], [VM], VM, [], 2**20, 2**20)
+        return call(preds_kernel, shape(*dims), [parts], [VM], VM, [], 2**20, 2**20, "preds")
 
     def gram_of(first, parts, prec_cut, value_cut):
         return call(
@@ -509,6 +548,7 @@
             [pltpu.VMEM((NMEM, CHUNK // 128, MEM, 128), F32)],
             2 * M * M * CHUNK,
             4 * M * CHUNK,
+            "gram",
         )
 
     def more(carry):
@@ -523,6 +563,7 @@
             [PRESSED, FOUND],
             BIG,
             8 * BIG,
+            "more",
         )
         group = group_preds(lax.all_gather(pred_n[0], "z"))
         groups = lax.all_gather(group, ("y", "core"))

time: 258 us -> 261 us (1.012)
  Pallas kernels: 38.5 us -> 41.6 us
    ppermute x1, waiting for transfers between devices: 0.01 us -> 4.85 us  [body(): lax.ppermute(first, 'x', down)]
    ppermute x1, waiting for transfers between devices: 3.81 us -> 0.01 us  [body(): s_left = lax.ppermute(sources[:, DEPTH - HALO:], 'x', up)]
    pallas_call x7, Pallas kernels: 38.5 us -> 41.6 us  [call(): pl.pallas_call(kernel, out_shape=outs, in_specs=specs, out_specs=out_spec...]
    unnamed x23 -> x15, local copies, waits for them, and re-layouts: 7.06 us -> 6.75 us
  transfers between devices with their start and end apart: 32 -> 32, of which waited for: 9 -> 9; matrix products, arithmetic and copies ran while one was open for 6% -> 5% of each run, Pallas kernels for 8% -> 8%
where the time goes in v1:
time: 261 us; the launch traced here: 258 us
  waiting for transfers between devices  101 us (39%)
  starting transfers between devices  65 us (25%)
  Pallas kernels  41.6 us (16%)
  blocking collectives  28.3 us (11%)
  local copies, waits for them, and re-layouts  11.6 us (4%)
  other arithmetic  6.97 us (3%)
  between operations  2.83 us (1%)
    ppermute x14, waiting for transfers between devices, shift_from(): lax.ppermute(array, axis, [((i + by) % size, i) for i in range(size)])  90.5 us
    pallas_call x7, Pallas kernels, call(): pl.pallas_call(kernel, out_shape=outs, in_specs=specs, out_specs=out_spec...  41.6 us
    ppermute x14, starting transfers between devices, shift_from(): lax.ppermute(array, axis, [((i + by) % size, i) for i in range(size)])  32.3 us
    all_to_all x2, blocking collectives, exchange(): return lax.all_to_all(copies, axis, 0, 0, tiled=True)  28.3 us
    all_to_all x2, starting transfers between devices, exchange(): return lax.all_to_all(copies, axis, 0, 0, tiled=True)  11.2 us
    ppermute x7, starting transfers between devices, round_mem(): parts.append(lax.ppermute(array, ('y', 'core'), pairs))  8.32 us
    unnamed x15, local copies, waits for them, and re-layouts  6.75 us
    sort x1, other arithmetic, body(): lax.sort((obs_cells, obs_prec, obs_values), num_keys=1)  5.94 us
  transfers between devices with their start and end apart: 32, of which 9 were waited for; matrix products, arithmetic and copies ran while one was open for 5% of the time, Pallas kernels for 8%

profile of v1, /device:TPU:64, one launch (start us, length us, event | category | flops | bytes accessed | tf_op | source)
XLA Modules:
  0.0 258.3 jit_solution(12162006765613246673)
XLA Ops:
  2.4 14.3 %all_to_all.20.strips = f32[8,2,8,256]{3,2,1,0:T(8,128)S(1)} all-to-all(f32[8,2,8,256]{3,2,1,0:T(8,128)} %shard_map.69), channel_id=1, replica_groups=mesh['x'=4,'z'=8,'y'=4,'core'=2] {'z'}, dimensions={0} | all-to-all | bytes 262144 | tf_op jit(solution)/shard_map/all_to_all | solution.py:407
  17.8 4.5 %all-to-all-start.1 = ((f32[8,16,8,256]{3,2,1,0:T(8,128)}), f32[8,16,8,256]{3,2,1,0:T(8,128)S(1)}, u32[]{:S(2)}, u32[]{:S(2)}) async-start(f32[8,16,8,256]{3,2,1,0:T(8,128)} %copy-done.1), calls=%async_computation.1 | async-start | bytes 2097152 | tf_op jit(solution)/shard_map/all_to_all | solution.py:407
  26.0 4.6 %collective-permute-start.4 = (f32[2,2,64,256]{3,2,1,0:T(8,128)}, f32[2,2,64,256]{3,2,1,0:T(8,128)}, u32[]{:S(2)}, u32[]{:S(2)}) collective-permute-start(f32[2,2,64,256]{3,2,1,0:T(8,128)} %get-tuple-element.189), channel_id=1, source_target_pairs={{40,0},{48,8},{56,16},{0,24},{8,32},{16,40},{24,48},{32,56},{41,1}... | collective-permute-start | bytes 786440 | tf_op jit(solution)/shard_map/ppermute | solution.py:403
  31.1 4.3 %collective-permute-start.2 = (f32[2,2,64,256]{3,2,1,0:T(8,128)}, f32[2,2,64,256]{3,2,1,0:T(8,128)}, u32[]{:S(2)}, u32[]{:S(2)}) collective-permute-start(f32[2,2,64,256]{3,2,1,0:T(8,128)} %get-tuple-element.191), channel_id=1, source_target_pairs={{24,0},{32,8},{40,16},{48,24},{56,32},{0,40},{8,48},{16,56},{25,1}... | collective-permute-start | bytes 786440 | tf_op jit(solution)/shard_map/ppermute | solution.py:403
  35.5 5.9 %sort.31 = (s32[4096]{0:T(1024)S(1)}, f32[4096]{0:T(1024)S(1)}, f32[4096]{0:T(1024)S(1)}, s32[4096]{0:T(1024)}) sort(s32[4096]{0:T(1024)S(1)} %copy-done.4, f32[4096]{0:T(1024)S(1)} %copy-done.5, f32[4096]{0:T(1024)S(1)} %copy-done.6, s32[4096]{0:T(1024)S(1)} %iota.26), dimensions={0}, to_apply=%region_0.0 | sort | flops 49152 | bytes 131072 | tf_op jit(solution)/shard_map/sort | solution.py:488
  41.4 1.6 collective-permute-start.1
  43.0 10.1 %collective-permute-start = (f32[2,2,64,256]{3,2,1,0:T(8,128)}, f32[2,2,64,256]{3,2,1,0:T(8,128)S(1)}, u32[]{:S(2)}, u32[]{:S(2)}) collective-permute-start(f32[2,2,64,256]{3,2,1,0:T(8,128)} %get-tuple-element.193), channel_id=1, source_target_pairs={{8,0},{16,8},{24,16},{32,24},{40,32},{48,40},{56,48},{0,56},{9,1},... | collective-permute-start | bytes 786440 | tf_op jit(solution)/shard_map/ppermute | solution.py:403
  53.2 22.2 %collective-permute-done.4.refs_5_ = f32[2,2,64,256]{3,2,1,0:T(8,128)} collective-permute-done((f32[2,2,64,256]{3,2,1,0:T(8,128)}, f32[2,2,64,256]{3,2,1,0:T(8,128)}, u32[]{:S(2)}, u32[]{:S(2)}) %collective-permute-start.4) | collective-permute-done | bytes 262176 | tf_op jit(solution)/shard_map/ppermute | solution.py:403
  75.5 2.4 collective-permute-done.refs_1_
  77.8 3.6 %shard_map.68 = (f32[2,16,64,256]{3,2,1,0:T(8,128)}, f32[2,4,64,256]{3,2,1,0:T(8,128)}, f32[2,4,64,256]{3,2,1,0:T(8,128)}) custom-call(s32[1]{0:T(128)} %bitcast.4.where, f32[2,2,64,256]{3,2,1,0:T(8,128)S(1)} %get-tuple-element.194.refs_0_, f32[2,2,64,256]{3,2,1,0:T(8,128)S(1)} %collective-permute-done.refs_1_, ...), custom_call_target="tpu_custom_call" | custom-call | flops 2097152 | bytes 6291456 | tf_op jit(solution)/shard_map/pallas_call | solution.py:45
  81.4 4.2 %collective-permute-start.7 = (f32[2,4,64,256]{3,2,1,0:T(8,128)}, f32[2,4,64,256]{3,2,1,0:T(8,128)}, u32[]{:S(2)}, u32[]{:S(2)}) collective-permute-start(f32[2,4,64,256]{3,2,1,0:T(8,128)} %get-tuple-element.145), channel_id=1, source_target_pairs={{0,64},{64,128},{128,192},{1,65},{65,129},{129,193},{2,66},{66,130... | collective-permute-start | bytes 1572872 | tf_op jit(solution)/shard_map/ppermute | solution.py:531
  89.0 5.9 %collective-permute-start.9 = (f32[8,4,8,256]{3,2,1,0:T(8,128)}, f32[8,4,8,256]{3,2,1,0:T(8,128)}, u32[]{:S(2)}, u32[]{:S(2)}) collective-permute-start(f32[8,4,8,256]{3,2,1,0:T(8,128)} %get-tuple-element.196), channel_id=1, source_target_pairs={{0,64},{64,128},{128,192},{1,65},{65,129},{129,193},{2,66},{66,130... | collective-permute-start | bytes 786440 | tf_op jit(solution)/shard_map/ppermute | solution.py:532
  97.8 4.9 %collective-permute-done.8.hr_ref = f32[2,4,64,256]{3,2,1,0:T(8,128)} collective-permute-done((f32[2,4,64,256]{3,2,1,0:T(8,128)}, f32[2,4,64,256]{3,2,1,0:T(8,128)}, u32[]{:S(2)}, u32[]{:S(2)}) %collective-permute-start.8) | collective-permute-done | bytes 524320 | tf_op jit(solution)/shard_map/ppermute | solution.py:531
  102.6 3.4 %collective-permute-done.10.sr_ref = f32[8,4,8,256]{3,2,1,0:T(8,128)S(1)} collective-permute-done((f32[8,4,8,256]{3,2,1,0:T(8,128)}, f32[8,4,8,256]{3,2,1,0:T(8,128)S(1)}, u32[]{:S(2)}, u32[]{:S(2)}) %collective-permute-start.10) | collective-permute-done | bytes 262176 | tf_op jit(solution)/shard_map/ppermute | solution.py:533
  106.0 1.6 copy-done.2
  107.6 19.1 %shard_map.71 = (f32[8,2,2,64,256]{4,3,2,1,0:T(8,128)}, f32[8,10,2,128]{3,2,1,0:T(2,128)S(1)}) custom-call(s32[4]{0:T(128)S(1)} %pad_add_fusion.1.where, s32[1280]{0:T(1024)S(1)} %get-tuple-element.198.spots, s32[1280]{0:T(1024)S(1)} %get-tuple-element.197.lanes, f32[2,16,64,256]{3,2,1,0:T(8,128)S(1)} %copy-done.2, ...), custom_call_target="tpu_custom_call" | custom-call | flops 33554432 | bytes 8388608 | tf_op jit(solution)/shard_map/pallas_call | solution.py:45
  126.7 13.9 %all_to_all.21.parts = f32[8,10,2,128]{3,2,1,0:T(2,128)S(1)} all-to-all(f32[8,10,2,128]{3,2,1,0:T(2,128)S(1)} %get-tuple-element.148), channel_id=1, replica_groups=mesh['x'=4,'z'=8,'y'=4,'core'=2] {'z'}, dimensions={0} | all-to-all | bytes 163840 | tf_op jit(solution)/shard_map/all_to_all | solution.py:407
  140.9 1.7 collective-permute-start.16
  142.6 2.4 collective-permute-start.15
  145.0 1.9 collective-permute-start.14
  147.2 1.6 collective-permute-start.12
  149.1 6.7 %all-to-all-start.2 = ((f32[16,2,64,256]{3,2,1,0:T(8,128)}), f32[16,2,64,256]{3,2,1,0:T(8,128)}, u32[]{:S(2)}, u32[]{:S(2)}) async-start(f32[16,2,64,256]{3,2,1,0:T(8,128)} %bitcast.17), calls=%async_computation.2 | async-start | bytes 4194304 | tf_op jit(solution)/shard_map/all_to_all | solution.py:407
  155.9 1.6 collective-permute-start.21
  162.0 2.5 collective-permute-start.18
  164.5 39.1 %collective-permute-done.21.refs_1_ = f32[16,2,64,256]{3,2,1,0:T(8,128)} collective-permute-done((f32[16,2,64,256]{3,2,1,0:T(8,128)S(1)}, f32[16,2,64,256]{3,2,1,0:T(8,128)}, u32[]{:S(2)}, u32[]{:S(2)}) %collective-permute-start.21) | collective-permute-done | bytes 2097184 | tf_op jit(solution)/shard_map/ppermute | solution.py:403
  203.6 1.3 slice.80
  205.8 1.9 collective-permute-start.23
  209.7 21.1 %collective-permute-done.23.refs_3_ = f32[8,2,64,256]{3,2,1,0:T(8,128)S(1)} collective-permute-done((f32[8,2,64,256]{3,2,1,0:T(8,128)S(1)}, f32[8,2,64,256]{3,2,1,0:T(8,128)S(1)}, u32[]{:S(2)}, u32[]{:S(2)}) %collective-permute-start.23) | collective-permute-done | bytes 1048608 | tf_op jit(solution)/shard_map/ppermute | solution.py:403
  230.8 4.8 %collective-permute-done.24.refs_4_ = f32[8,2,64,256]{3,2,1,0:T(8,128)S(1)} collective-permute-done((f32[8,2,64,256]{3,2,1,0:T(8,128)S(1)}, f32[8,2,64,256]{3,2,1,0:T(8,128)S(1)}, u32[]{:S(2)}, u32[]{:S(2)}) %collective-permute-start.24) | collective-permute-done | bytes 1048608 | tf_op jit(solution)/shard_map/ppermute | solution.py:403
  235.6 2.6 %collective-permute-done.29.refs_9_ = f32[8,2,64,256]{3,2,1,0:T(8,128)S(1)} collective-permute-done((f32[8,2,64,256]{3,2,1,0:T(8,128)S(1)}, f32[8,2,64,256]{3,2,1,0:T(8,128)S(1)}, u32[]{:S(2)}, u32[]{:S(2)}) %collective-permute-start.29) | collective-permute-done | bytes 1048608 | tf_op jit(solution)/shard_map/ppermute | solution.py:456
  238.3 16.9 %shard_map.74 = f32[16,2,64,256]{3,2,1,0:T(8,128)} custom-call(s32[4]{0:T(128)S(1)} %pad_add_fusion.1.where, f32[136,128]{1,0:T(8,128)S(1)} %get-tuple-element.151.g0, f32[136,128]{1,0:T(8,128)S(1)} %collective-permute-done.18.g1, f32[136,128]{1,0:T(8,128)S(1)} %collective-permute-done.19.g2, f32[136,128]{1,0:T(8,128)S(1)} %collective-permute-done.20.g3, ...), custom_call_target="tpu_custom_call" | custom-call | flops 134217728 | bytes 16777216 | tf_op jit(solution)/shard_map/pallas_call | solution.py:45
  255.2 3.1 %copy.14 = f32[16,2,64,256]{3,2,1,0:T(8,128)} copy(f32[16,2,64,256]{3,2,1,0:T(8,128)} %all-to-all-done.2) | data formatting | bytes 4194304
  (72 shorter events, 19.6 us)
Async XLA Ops:
  17.8 69.1 %all-to-all-start.1 = ((f32[8,16,8,256]{3,2,1,0:T(8,128)}), f32[8,16,8,256]{3,2,1,0:T(8,128)S(1)}, u32[]{:S(2)}, u32[]{:S(2)}) async-start(f32[8,16,8,256]{3,2,1,0:T(8,128)} %copy-done.1), calls=%async_computation.1 | async-start | bytes 2097152 | tf_op jit(solution)/shard_map/all_to_all | solution.py:407
  23.6 17.8 %collective-permute-start.6 = (f32[2,2,64,256]{3,2,1,0:T(8,128)}, f32[2,2,64,256]{3,2,1,0:T(8,128)}, u32[]{:S(2)}, u32[]{:S(2)}) collective-permute-start(f32[2,2,64,256]{3,2,1,0:T(8,128)} %get-tuple-element.187), channel_id=1, source_target_pairs={{56,0},{0,8},{8,16},{16,24},{24,32},{32,40},{40,48},{48,56},{57,1}... | collective-permute-start | bytes 786440 | tf_op jit(solution)/shard_map/ppermute | solution.py:403
  24.6 18.4 %collective-permute-start.5 = (f32[2,2,64,256]{3,2,1,0:T(8,128)}, f32[2,2,64,256]{3,2,1,0:T(8,128)}, u32[]{:S(2)}, u32[]{:S(2)}) collective-permute-start(f32[2,2,64,256]{3,2,1,0:T(8,128)} %get-tuple-element.188), channel_id=1, source_target_pairs={{48,0},{56,8},{0,16},{8,24},{16,32},{24,40},{32,48},{40,56},{49,1}... | collective-permute-start | bytes 786440 | tf_op jit(solution)/shard_map/ppermute | solution.py:403
  26.0 49.5 %collective-permute-start.4 = (f32[2,2,64,256]{3,2,1,0:T(8,128)}, f32[2,2,64,256]{3,2,1,0:T(8,128)}, u32[]{:S(2)}, u32[]{:S(2)}) collective-permute-start(f32[2,2,64,256]{3,2,1,0:T(8,128)} %get-tuple-element.189), channel_id=1, source_target_pairs={{40,0},{48,8},{56,16},{0,24},{8,32},{16,40},{24,48},{32,56},{41,1}... | collective-permute-start | bytes 786440 | tf_op jit(solution)/shard_map/ppermute | solution.py:403
  30.6 44.9 %collective-permute-start.3 = (f32[2,2,64,256]{3,2,1,0:T(8,128)}, f32[2,2,64,256]{3,2,1,0:T(8,128)}, u32[]{:S(2)}, u32[]{:S(2)}) collective-permute-start(f32[2,2,64,256]{3,2,1,0:T(8,128)} %get-tuple-element.190), channel_id=1, source_target_pairs={{32,0},{40,8},{48,16},{56,24},{0,32},{8,40},{16,48},{24,56},{33,1}... | collective-permute-start | bytes 786440 | tf_op jit(solution)/shard_map/ppermute | solution.py:403
  31.1 44.3 %collective-permute-start.2 = (f32[2,2,64,256]{3,2,1,0:T(8,128)}, f32[2,2,64,256]{3,2,1,0:T(8,128)}, u32[]{:S(2)}, u32[]{:S(2)}) collective-permute-start(f32[2,2,64,256]{3,2,1,0:T(8,128)} %get-tuple-element.191), channel_id=1, source_target_pairs={{24,0},{32,8},{40,16},{48,24},{56,32},{0,40},{8,48},{16,56},{25,1}... | collective-permute-start | bytes 786440 | tf_op jit(solution)/shard_map/ppermute | solution.py:403
  41.4 34.0 %collective-permute-start.1 = (f32[2,2,64,256]{3,2,1,0:T(8,128)}, f32[2,2,64,256]{3,2,1,0:T(8,128)S(1)}, u32[]{:S(2)}, u32[]{:S(2)}) collective-permute-start(f32[2,2,64,256]{3,2,1,0:T(8,128)} %get-tuple-element.192), channel_id=1, source_target_pairs={{16,0},{24,8},{32,16},{40,24},{48,32},{56,40},{0,48},{8,56},{17,1}... | collective-permute-start | bytes 786440 | tf_op jit(solution)/shard_map/ppermute | solution.py:403
  43.0 34.8 %collective-permute-start = (f32[2,2,64,256]{3,2,1,0:T(8,128)}, f32[2,2,64,256]{3,2,1,0:T(8,128)S(1)}, u32[]{:S(2)}, u32[]{:S(2)}) collective-permute-start(f32[2,2,64,256]{3,2,1,0:T(8,128)} %get-tuple-element.193), channel_id=1, source_target_pairs={{8,0},{16,8},{24,16},{32,24},{40,32},{48,40},{56,48},{0,56},{9,1},... | collective-permute-start | bytes 786440 | tf_op jit(solution)/shard_map/ppermute | solution.py:403
  81.4 16.4 %collective-permute-start.7 = (f32[2,4,64,256]{3,2,1,0:T(8,128)}, f32[2,4,64,256]{3,2,1,0:T(8,128)}, u32[]{:S(2)}, u32[]{:S(2)}) collective-permute-start(f32[2,4,64,256]{3,2,1,0:T(8,128)} %get-tuple-element.145), channel_id=1, source_target_pairs={{0,64},{64,128},{128,192},{1,65},{65,129},{129,193},{2,66},{66,130... | collective-permute-start | bytes 1572872 | tf_op jit(solution)/shard_map/ppermute | solution.py:531
  85.6 17.0 %collective-permute-start.8 = (f32[2,4,64,256]{3,2,1,0:T(8,128)}, f32[2,4,64,256]{3,2,1,0:T(8,128)}, u32[]{:S(2)}, u32[]{:S(2)}) collective-permute-start(f32[2,4,64,256]{3,2,1,0:T(8,128)} %get-tuple-element.146), channel_id=1, source_target_pairs={{64,0},{128,64},{192,128},{65,1},{129,65},{193,129},{66,2},{130,66... | collective-permute-start | bytes 1572872 | tf_op jit(solution)/shard_map/ppermute | solution.py:531
  87.8 18.3 %collective-permute-start.10 = (f32[8,4,8,256]{3,2,1,0:T(8,128)}, f32[8,4,8,256]{3,2,1,0:T(8,128)S(1)}, u32[]{:S(2)}, u32[]{:S(2)}) collective-permute-start(f32[8,4,8,256]{3,2,1,0:T(8,128)} %get-tuple-element.195), channel_id=1, source_target_pairs={{64,0},{128,64},{192,128},{65,1},{129,65},{193,129},{66,2},{130,66... | collective-permute-start | bytes 786440 | tf_op jit(solution)/shard_map/ppermute | solution.py:533
  89.0 17.0 %collective-permute-start.9 = (f32[8,4,8,256]{3,2,1,0:T(8,128)}, f32[8,4,8,256]{3,2,1,0:T(8,128)}, u32[]{:S(2)}, u32[]{:S(2)}) collective-permute-start(f32[8,4,8,256]{3,2,1,0:T(8,128)} %get-tuple-element.196), channel_id=1, source_target_pairs={{0,64},{64,128},{128,192},{1,65},{65,129},{129,193},{2,66},{66,130... | collective-permute-start | bytes 786440 | tf_op jit(solution)/shard_map/ppermute | solution.py:532
  140.6 6.6 %collective-permute-start.17 = (f32[10,16,128]{2,1,0:T(8,128)S(1)}, f32[10,16,128]{2,1,0:T(8,128)S(1)}, u32[]{:S(2)}, u32[]{:S(2)}) collective-permute-start(f32[10,16,128]{2,1,0:T(8,128)S(1)} %shard_map.72.refs_0_), channel_id=1, source_target_pairs={{7,0},{6,1},{1,2},{0,3},{3,4},{2,5},{5,6},{4,7},{15,8},{14,9},{9,1... | collective-permute-start | bytes 245768 | tf_op jit(solution)/shard_map/ppermute | solution.py:443
  140.9 7.9 %collective-permute-start.16 = (f32[10,16,128]{2,1,0:T(8,128)S(1)}, f32[10,16,128]{2,1,0:T(8,128)S(1)}, u32[]{:S(2)}, u32[]{:S(2)}) collective-permute-start(f32[10,16,128]{2,1,0:T(8,128)S(1)} %shard_map.72.refs_0_), channel_id=1, source_target_pairs={{6,0},{7,1},{0,2},{1,3},{2,4},{3,5},{4,6},{5,7},{14,8},{15,9},{8,1... | collective-permute-start | bytes 245768 | tf_op jit(solution)/shard_map/ppermute | solution.py:443
  142.6 13.2 %collective-permute-start.15 = (f32[10,16,128]{2,1,0:T(8,128)S(1)}, f32[10,16,128]{2,1,0:T(8,128)S(1)}, u32[]{:S(2)}, u32[]{:S(2)}) collective-permute-start(f32[10,16,128]{2,1,0:T(8,128)S(1)} %shard_map.72.refs_0_), channel_id=1, source_target_pairs={{5,0},{4,1},{7,2},{6,3},{1,4},{0,5},{3,6},{2,7},{13,8},{12,9},{15,... | collective-permute-start | bytes 245768 | tf_op jit(solution)/shard_map/ppermute | solution.py:443
  145.0 12.5 %collective-permute-start.14 = (f32[10,16,128]{2,1,0:T(8,128)S(1)}, f32[10,16,128]{2,1,0:T(8,128)S(1)}, u32[]{:S(2)}, u32[]{:S(2)}) collective-permute-start(f32[10,16,128]{2,1,0:T(8,128)S(1)} %shard_map.72.refs_0_), channel_id=1, source_target_pairs={{4,0},{5,1},{6,2},{7,3},{0,4},{1,5},{2,6},{3,7},{12,8},{13,9},{14,... | collective-permute-start | bytes 245768 | tf_op jit(solution)/shard_map/ppermute | solution.py:443
  147.0 10.9 %collective-permute-start.13 = (f32[10,16,128]{2,1,0:T(8,128)S(1)}, f32[10,16,128]{2,1,0:T(8,128)S(1)}, u32[]{:S(2)}, u32[]{:S(2)}) collective-permute-start(f32[10,16,128]{2,1,0:T(8,128)S(1)} %shard_map.72.refs_0_), channel_id=1, source_target_pairs={{3,0},{2,1},{5,2},{4,3},{7,4},{6,5},{1,6},{0,7},{11,8},{10,9},{13,... | collective-permute-start | bytes 245768 | tf_op jit(solution)/shard_map/ppermute | solution.py:443
  147.2 10.7 %collective-permute-start.12 = (f32[10,16,128]{2,1,0:T(8,128)S(1)}, f32[10,16,128]{2,1,0:T(8,128)S(1)}, u32[]{:S(2)}, u32[]{:S(2)}) collective-permute-start(f32[10,16,128]{2,1,0:T(8,128)S(1)} %shard_map.72.refs_0_), channel_id=1, source_target_pairs={{2,0},{3,1},{4,2},{5,3},{6,4},{7,5},{0,6},{1,7},{10,8},{11,9},{12,... | collective-permute-start | bytes 245768 | tf_op jit(solution)/shard_map/ppermute | solution.py:443
  148.8 9.0 %collective-permute-start.11 = (f32[10,16,128]{2,1,0:T(8,128)S(1)}, f32[10,16,128]{2,1,0:T(8,128)S(1)}, u32[]{:S(2)}, u32[]{:S(2)}) collective-permute-start(f32[10,16,128]{2,1,0:T(8,128)S(1)} %shard_map.72.refs_0_), channel_id=1, source_target_pairs={{1,0},{0,1},{3,2},{2,3},{5,4},{4,5},{7,6},{6,7},{9,8},{8,9},{11,10... | collective-permute-start | bytes 245768 | tf_op jit(solution)/shard_map/ppermute | solution.py:443
  149.1 106.0 %all-to-all-start.2 = ((f32[16,2,64,256]{3,2,1,0:T(8,128)}), f32[16,2,64,256]{3,2,1,0:T(8,128)}, u32[]{:S(2)}, u32[]{:S(2)}) async-start(f32[16,2,64,256]{3,2,1,0:T(8,128)} %bitcast.17), calls=%async_computation.2 | async-start | bytes 4194304 | tf_op jit(solution)/shard_map/all_to_all | solution.py:407
  155.9 47.7 %collective-permute-start.21 = (f32[16,2,64,256]{3,2,1,0:T(8,128)S(1)}, f32[16,2,64,256]{3,2,1,0:T(8,128)}, u32[]{:S(2)}, u32[]{:S(2)}) collective-permute-start(f32[16,2,64,256]{3,2,1,0:T(8,128)S(1)} %copy-done), channel_id=1, source_target_pairs={{2,0},{4,2},{6,4},{0,6},{3,1},{5,3},{7,5},{1,7},{10,8},{12,10},{14... | collective-permute-start | bytes 6291464 | tf_op jit(solution)/shard_map/ppermute | solution.py:403
  157.5 48.3 %collective-permute-start.22 = (f32[16,2,64,256]{3,2,1,0:T(8,128)S(1)}, f32[16,2,64,256]{3,2,1,0:T(8,128)}, u32[]{:S(2)}, u32[]{:S(2)}) collective-permute-start(f32[16,2,64,256]{3,2,1,0:T(8,128)S(1)} %copy-done), channel_id=1, source_target_pairs={{6,0},{0,2},{2,4},{4,6},{7,1},{1,3},{3,5},{5,7},{14,8},{8,10},{10,... | collective-permute-start | bytes 6291464 | tf_op jit(solution)/shard_map/ppermute | solution.py:403
  159.9 49.2 %collective-permute-start.20 = (f32[136,128]{1,0:T(8,128)S(1)}, f32[136,128]{1,0:T(8,128)S(1)}, u32[]{:S(2)}, u32[]{:S(2)}) collective-permute-start(f32[136,128]{1,0:T(8,128)S(1)} %get-tuple-element.151.g0), channel_id=1, source_target_pairs={{192,0},{0,64},{64,128},{128,192},{193,1},{1,65},{65,129},{129,193... | collective-permute-start | bytes 208904 | tf_op jit(solution)/shard_map/ppermute | solution.py:403
  161.0 48.3 %collective-permute-start.19 = (f32[136,128]{1,0:T(8,128)S(1)}, f32[136,128]{1,0:T(8,128)S(1)}, u32[]{:S(2)}, u32[]{:S(2)}) collective-permute-start(f32[136,128]{1,0:T(8,128)S(1)} %get-tuple-element.151.g0), channel_id=1, source_target_pairs={{128,0},{192,64},{0,128},{64,192},{129,1},{193,65},{1,129},{65,193... | collective-permute-start | bytes 208904 | tf_op jit(solution)/shard_map/ppermute | solution.py:403
  162.0 47.5 %collective-permute-start.18 = (f32[136,128]{1,0:T(8,128)S(1)}, f32[136,128]{1,0:T(8,128)S(1)}, u32[]{:S(2)}, u32[]{:S(2)}) collective-permute-start(f32[136,128]{1,0:T(8,128)S(1)} %get-tuple-element.151.g0), channel_id=1, source_target_pairs={{64,0},{128,64},{192,128},{0,192},{65,1},{129,65},{193,129},{1,193... | collective-permute-start | bytes 208904 | tf_op jit(solution)/shard_map/ppermute | solution.py:403
  203.6 32.0 %collective-permute-start.25 = (f32[16,2,64,256]{3,2,1,0:T(8,128)S(1)}, f32[16,2,64,256]{3,2,1,0:T(8,128)S(1)}, u32[]{:S(2)}, u32[]{:S(2)}) collective-permute-start(f32[16,2,64,256]{3,2,1,0:T(8,128)S(1)} %copy-done), channel_id=1, source_target_pairs={{0,1},{1,0},{2,3},{3,2},{4,5},{5,4},{6,7},{7,6},{8,9},{9,8},{10,11... | collective-permute-start | bytes 6291464 | tf_op jit(solution)/shard_map/ppermute | solution.py:456
  205.8 25.0 %collective-permute-start.23 = (f32[8,2,64,256]{3,2,1,0:T(8,128)S(1)}, f32[8,2,64,256]{3,2,1,0:T(8,128)S(1)}, u32[]{:S(2)}, u32[]{:S(2)}) collective-permute-start(f32[8,2,64,256]{3,2,1,0:T(8,128)S(1)} %slice.80), channel_id=1, source_target_pairs={{2,0},{4,2},{6,4},{0,6},{3,1},{5,3},{7,5},{1,7},{10,8},{12,10},{14... | collective-permute-start | bytes 3145736 | tf_op jit(solution)/shard_map/ppermute | solution.py:403
  209.0 26.6 %collective-permute-start.24 = (f32[8,2,64,256]{3,2,1,0:T(8,128)S(1)}, f32[8,2,64,256]{3,2,1,0:T(8,128)S(1)}, u32[]{:S(2)}, u32[]{:S(2)}) collective-permute-start(f32[8,2,64,256]{3,2,1,0:T(8,128)S(1)} %slice.81), channel_id=1, source_target_pairs={{6,0},{0,2},{2,4},{4,6},{7,1},{1,3},{3,5},{5,7},{14,8},{8,10},{10,... | collective-permute-start | bytes 3145736 | tf_op jit(solution)/shard_map/ppermute | solution.py:403
  209.2 26.4 %collective-permute-start.26 = (f32[16,2,64,256]{3,2,1,0:T(8,128)}, f32[16,2,64,256]{3,2,1,0:T(8,128)S(1)}, u32[]{:S(2)}, u32[]{:S(2)}) collective-permute-start(f32[16,2,64,256]{3,2,1,0:T(8,128)} %collective-permute-done.21.refs_1_), channel_id=1, source_target_pairs={{0,1},{1,0},{2,3},{3,2},{4,5},{5,4},{6,7},{7,6},{8,9},{9,8},{10,11... | collective-permute-start | bytes 6291464 | tf_op jit(solution)/shard_map/ppermute | solution.py:456
  209.5 28.8 %collective-permute-start.27 = (f32[16,2,64,256]{3,2,1,0:T(8,128)}, f32[16,2,64,256]{3,2,1,0:T(8,128)S(1)}, u32[]{:S(2)}, u32[]{:S(2)}) collective-permute-start(f32[16,2,64,256]{3,2,1,0:T(8,128)} %collective-permute-done.22.refs_2_), channel_id=1, source_target_pairs={{0,1},{1,0},{2,3},{3,2},{4,5},{5,4},{6,7},{7,6},{8,9},{9,8},{10,11... | collective-permute-start | bytes 6291464 | tf_op jit(solution)/shard_map/ppermute | solution.py:456
  230.8 4.8 %collective-permute-start.28 = (f32[8,2,64,256]{3,2,1,0:T(8,128)S(1)}, f32[8,2,64,256]{3,2,1,0:T(8,128)S(1)}, u32[]{:S(2)}, u32[]{:S(2)}) collective-permute-start(f32[8,2,64,256]{3,2,1,0:T(8,128)S(1)} %collective-permute-done.23.refs_3_), channel_id=1, source_target_pairs={{0,1},{1,0},{2,3},{3,2},{4,5},{5,4},{6,7},{7,6},{8,9},{9,8},{10,11... | collective-permute-start | bytes 3145736 | tf_op jit(solution)/shard_map/ppermute | solution.py:456
  235.6 2.7 %collective-permute-start.29 = (f32[8,2,64,256]{3,2,1,0:T(8,128)S(1)}, f32[8,2,64,256]{3,2,1,0:T(8,128)S(1)}, u32[]{:S(2)}, u32[]{:S(2)}) collective-permute-start(f32[8,2,64,256]{3,2,1,0:T(8,128)S(1)} %collective-permute-done.24.refs_4_), channel_id=1, source_target_pairs={{0,1},{1,0},{2,3},{3,2},{4,5},{5,4},{6,7},{7,6},{8,9},{9,8},{10,11... | collective-permute-start | bytes 3145736 | tf_op jit(solution)/shard_map/ppermute | solution.py:456
  (7 other events, 64.8 us)

commit v2 on v1

--- a/solution.py
+++ b/solution.py
@@ -38,7 +38,7 @@
     return jax.ShapeDtypeStruct(dims, F32)
 
 
-LIMITS = {"roots": 16, "sweeps": 32, "analysis": 32, "more": 16}
+LIMITS = {"ends": 8, "sweeps": 32, "analysis": 32, "more": 16}
 
 
 def call(kernel, outs, ins, specs, out_specs, scratch, flops, moved, name):
@@ -53,25 +53,30 @@
     )(*ins)
 
 
-def roots_kernel(where, *refs):
-    parts, (h_ref, first_ref, last_ref, buffer, h, sems, out_sems) = refs[:NZ], refs[NZ:]
-    copies = [pltpu.make_async_copy(parts[d], buffer.at[d], sems.at[d]) for d in range(NZ)]
-    for copy in copies:
-        copy.start()
-    results = []
-    for d in range(NZ):
-        copies[d].wait()
-        slab = (where[0] + d) & (NZ - 1)
+def root(value):
+    return jnp.exp(0.5 * value)
+
+
+def edges_kernel(where, *refs):
+    parts, (first_ref, last_ref, buffer, sems) = refs[:NZ], refs[NZ:]
+    ends = HALO // LAY
+
+    def for_ends(act):
+        for d in range(NZ):
+            slab = (where[0] + d) & (NZ - 1)
+            spot = jnp.where(slab < ends, slab, slab - (NZ - 2 * ends))
+
+            @pl.when((slab < ends) | (slab >= NZ - ends))
+            def _():
+                act(pltpu.make_async_copy(parts[d], buffer.at[spot], sems.at[spot]))
+
+    for_ends(lambda copy: copy.start())
+    for_ends(lambda copy: copy.wait())
+    for spot in range(ends):
         for m in range(SUB):
-            for a in range(LAY):
-                h[m, slab * LAY + a] = jnp.exp(0.5 * buffer[d, m, a])
-        layers = pl.ds(slab * LAY, LAY)
-        results.append(pltpu.make_async_copy(h.at[:, layers], h_ref.at[:, layers], out_sems.at[d]))
-        results[-1].start()
-    first_ref[...] = h[:, 0:HALO]
-    last_ref[...] = h[:, DEPTH - HALO : DEPTH]
-    for result in results:
-        result.wait()
+            layers = pl.ds(spot * LAY, LAY)
+            first_ref[m, layers] = root(buffer[spot, m])
+            last_ref[m, layers] = root(buffer[ends + spot, m])
 
 
 TILES = [(i, half) for i in range(NY // 8) for half in range(NW // 128)]
@@ -141,24 +146,23 @@
         copies[copy] = out[...]
 
 
-def sweeps_kernel(where, spots, lanes, h_ref, hl_ref, hr_ref, s_mid, sl_ref, sr_ref, *refs):
-    out, pred_ref, h_all, s_ref, qs, qw, qb, qc, rest, weight, sums, band, *refs = refs
-    press, found, sems, in_sems, s_sems = refs
+def sweeps_kernel(where, spots, lanes, hl_ref, hr_ref, s_mid, sl_ref, sr_ref, *refs):
+    parts, refs = refs[:NZ], refs[NZ:]
+    out, pred_ref, h_all, raw, s_ref, qs, qw, qb, qc, rest, weight, sums, band, *refs = refs
+    press, found, sems, in_sems, h_sems, s_sems = refs
     cuts = [(0, HALO), (HALO, DEPTH), (HALO + DEPTH, HALO)]
 
-    def roots(m):
-        copies = []
-        for n, source in enumerate((hl_ref, h_ref, hr_ref)):
-            first, layers = cuts[n]
-            there = h_all.at[m, pl.ds(1 + first, layers)]
-            copies.append(pltpu.make_async_copy(source.at[m], there, in_sems.at[m, n]))
-        return copies
+    halos = []
+    for n, source in enumerate((hl_ref, hr_ref)):
+        there = h_all.at[:, pl.ds(1 + cuts[2 * n][0], HALO)]
+        halos.append(pltpu.make_async_copy(source, there, h_sems.at[n]))
+    arrivals = [pltpu.make_async_copy(parts[d], raw.at[d], in_sems.at[d]) for d in range(NZ)]
 
     strips = []
     for n, source in enumerate((sl_ref, s_mid, sr_ref)):
         there = s_ref.at[:, pl.ds(*cuts[n])]
         strips.append(pltpu.make_async_copy(source, there, s_sems.at[n]))
-    for copy in [*roots(0), *strips, *roots(1)]:
+    for copy in [*arrivals, *halos, *strips]:
         copy.start()
 
     def results(m):
@@ -177,26 +181,30 @@
     for m in range(SUB):
         h_all[m, 0] = jnp.zeros((NY, NW), F32)
         h_all[m, FULL + 1 : ROOM] = jnp.zeros((ROOM - FULL - 1, NY, NW), F32)
-    for copy in strips:
+    for copy in [*arrivals, *halos, *strips]:
         copy.wait()
 
     @pl.loop(0, SUB)
     def _(m):
-        for copy in roots(m):
-            copy.wait()
         h = h_all.at[m]
 
+        @pl.loop(0, NZ)
+        def _(d):
+            slab = (where[0] + d) & (NZ - 1)
+            for a in range(LAY):
+                h[1 + HALO + slab * LAY + a] = root(raw[d, m, a])
+
         def prepare(j):
-            root, near = near_sums(h, sums, j)
+            roots, near = near_sums(h, sums, j)
             for i, half in TILES:
                 t, spot = (i, half), (j, *tile(i, half))
-                inverse = 1.0 / (CPRESS + root[t] * near[t])
+                inverse = 1.0 / (CPRESS + roots[t] * near[t])
                 start = s_ref[i, j - 1, :, pl.ds(128 * half, 128)] * inverse
-                slope = root[t] * inverse
+                slope = roots[t] * inverse
                 rest[spot] = start
                 weight[spot] = slope
-                qs[spot] = root[t] * start
-                qw[spot] = root[t] * slope
+                qs[spot] = roots[t] * start
+                qw[spot] = roots[t] * slope
 
         def sweep_to(new, old):
             def step(j):
@@ -366,13 +374,14 @@
         sweeps_kernel,
         [PARTS, PRED],
         ins,
-        [SM] * 3 + [HBM] + [ANY] * 5,
+        [SM] * 3 + [ANY] * (5 + NZ),
         [HBM, VM],
-        [pltpu.VMEM((SUB, ROOM, NY, NW), F32), pltpu.VMEM((NMEM, FULL + 2, ROWS_OF, NW), F32)]
+        [pltpu.VMEM((SUB, ROOM, NY, NW), F32), pltpu.VMEM((NZ, SUB, LAY, NY, NW), F32)]
+        + [pltpu.VMEM((NMEM, FULL + 2, ROWS_OF, NW), F32)]
         + [pltpu.VMEM((ROOM, NY, NW), F32)] * 7
         + [pltpu.VMEM((NW, NW), jnp.bfloat16), PRESSED, FOUND]
         + [pltpu.SemaphoreType.DMA((SUB, HALVES, NZ))]
-        + [pltpu.SemaphoreType.DMA((SUB, 3)), pltpu.SemaphoreType.DMA((3,))],
+        + [pltpu.SemaphoreType.DMA((n,)) for n in (NZ, 2, 3)],
         64 * BIG,
         16 * BIG,
         "sweeps",
@@ -510,21 +519,19 @@
 
     where, spots_0, lanes_0, prec_0, values_0 = window(0)
     edge = shape(SUB, HALO, NY, NW)
-    h, first, last = call(
-        roots_kernel,
-        [pltpu.HBM((SUB, DEPTH, NY, NW), F32), edge, edge],
+    first, last = call(
+        edges_kernel,
+        [edge, edge],
         [jnp.reshape(z, (1,)).astype(jnp.int32), *parts],
         [SM] + [ANY] * NZ,
-        [HBM, VM, VM],
+        [VM, VM],
         [
-            pltpu.VMEM((NZ, SUB, LAY, NY, NW), F32),
-            pltpu.VMEM((SUB, DEPTH, NY, NW), F32),
-            pltpu.SemaphoreType.DMA((NZ,)),
-            pltpu.SemaphoreType.DMA((NZ,)),
+            pltpu.VMEM((2 * HALO // LAY, SUB, LAY, NY, NW), F32),
+            pltpu.SemaphoreType.DMA((2 * HALO // LAY,)),
         ],
+        BIG,
         4 * BIG,
-        12 * BIG,
-        "roots",
+        "ends",
     )
     up = [(i, i + 1) for i in range(NX - 1)]
     down = [(i + 1, i) for i in range(NX - 1)]
@@ -532,7 +539,9 @@
     s_left = lax.ppermute(sources[:, DEPTH - HALO :], "x", up)
     s_right = lax.ppermute(sources[:, :HALO], "x", down)
 
-    sent, pred = sweep(where, spots_0, lanes_0, h, h_left, h_right, sources, s_left, s_right)
+    sent, pred = sweep(
+        where, spots_0, lanes_0, h_left, h_right, sources, s_left, s_right, *parts
+    )
 
     def group_preds(parts):
         dims = (CHUNK // 128, MEM, 128)

time: 261 us -> 262 us (level)
    unnamed x15 -> x21, local copies, waits for them, and re-layouts: 6.75 us -> 7.07 us
where the time goes in v2:
time: 262 us; the launch traced here: 259 us
  waiting for transfers between devices  102 us (39%)
  starting transfers between devices  65 us (25%)
  Pallas kernels  41.9 us (16%)
  blocking collectives  28.1 us (11%)
  local copies, waits for them, and re-layouts  12 us (5%)
  other arithmetic  6.97 us (3%)
  between operations  2.7 us (1%)
    ppermute x14, waiting for transfers between devices, shift_from(): lax.ppermute(array, axis, [((i + by) % size, i) for i in range(size)])  90.4 us
    pallas_call x7, Pallas kernels, call(): pl.pallas_call(kernel, out_shape=outs, in_specs=specs, out_specs=out_spec...  41.9 us
    ppermute x14, starting transfers between devices, shift_from(): lax.ppermute(array, axis, [((i + by) % size, i) for i in range(size)])  32.3 us
    all_to_all x2, blocking collectives, exchange(): return lax.all_to_all(copies, axis, 0, 0, tiled=True)  28.1 us
    all_to_all x2, starting transfers between devices, exchange(): return lax.all_to_all(copies, axis, 0, 0, tiled=True)  11.2 us
    ppermute x7, starting transfers between devices, round_mem(): parts.append(lax.ppermute(array, ('y', 'core'), pairs))  8.32 us
    unnamed x21, local copies, waits for them, and re-layouts  7.07 us
    sort x1, other arithmetic, body(): lax.sort((obs_cells, obs_prec, obs_values), num_keys=1)  5.94 us
  transfers between devices with their start and end apart: 32, of which 9 were waited for; matrix products, arithmetic and copies ran while one was open for 5% of the time, Pallas kernels for 8%

profile of v2, /device:TPU:64, one launch (start us, length us, event | category | flops | bytes accessed | tf_op | source)
XLA Modules:
  0.0 258.9 jit_solution(16486656093694812022)
XLA Ops:
  2.4 14.3 %all_to_all.20.strips = f32[8,2,8,256]{3,2,1,0:T(8,128)S(1)} all-to-all(f32[8,2,8,256]{3,2,1,0:T(8,128)} %shard_map.69), channel_id=1, replica_groups=mesh['x'=4,'z'=8,'y'=4,'core'=2] {'z'}, dimensions={0} | all-to-all | bytes 262144 | tf_op jit(solution)/shard_map/all_to_all | solution.py:416
  17.8 4.5 %all-to-all-start.1 = ((f32[8,16,8,256]{3,2,1,0:T(8,128)}), f32[8,16,8,256]{3,2,1,0:T(8,128)S(1)}, u32[]{:S(2)}, u32[]{:S(2)}) async-start(f32[8,16,8,256]{3,2,1,0:T(8,128)} %copy-done.1), calls=%async_computation.1 | async-start | bytes 2097152 | tf_op jit(solution)/shard_map/all_to_all | solution.py:416
  25.9 4.6 %collective-permute-start.4 = (f32[2,2,64,256]{3,2,1,0:T(8,128)}, f32[2,2,64,256]{3,2,1,0:T(8,128)}, u32[]{:S(2)}, u32[]{:S(2)}) collective-permute-start(f32[2,2,64,256]{3,2,1,0:T(8,128)} %get-tuple-element.187), channel_id=1, source_target_pairs={{40,0},{48,8},{56,16},{0,24},{8,32},{16,40},{24,48},{32,56},{41,1}... | collective-permute-start | bytes 786440 | tf_op jit(solution)/shard_map/ppermute | solution.py:412
  31.1 4.3 %collective-permute-start.2 = (f32[2,2,64,256]{3,2,1,0:T(8,128)}, f32[2,2,64,256]{3,2,1,0:T(8,128)}, u32[]{:S(2)}, u32[]{:S(2)}) collective-permute-start(f32[2,2,64,256]{3,2,1,0:T(8,128)} %get-tuple-element.189), channel_id=1, source_target_pairs={{24,0},{32,8},{40,16},{48,24},{56,32},{0,40},{8,48},{16,56},{25,1}... | collective-permute-start | bytes 786440 | tf_op jit(solution)/shard_map/ppermute | solution.py:412
  35.5 5.9 %sort.31 = (s32[4096]{0:T(1024)S(1)}, f32[4096]{0:T(1024)S(1)}, f32[4096]{0:T(1024)S(1)}, s32[4096]{0:T(1024)}) sort(s32[4096]{0:T(1024)S(1)} %copy-done.7, f32[4096]{0:T(1024)S(1)} %copy-done.8, f32[4096]{0:T(1024)S(1)} %copy-done.9, s32[4096]{0:T(1024)S(1)} %iota.26), dimensions={0}, to_apply=%region_0.0 | sort | flops 49152 | bytes 131072 | tf_op jit(solution)/shard_map/sort | solution.py:497
  41.4 1.6 collective-permute-start.1
  43.0 10.1 %collective-permute-start = (f32[2,2,64,256]{3,2,1,0:T(8,128)}, f32[2,2,64,256]{3,2,1,0:T(8,128)S(1)}, u32[]{:S(2)}, u32[]{:S(2)}) collective-permute-start(f32[2,2,64,256]{3,2,1,0:T(8,128)} %get-tuple-element.191), channel_id=1, source_target_pairs={{8,0},{16,8},{24,16},{32,24},{40,32},{48,40},{56,48},{0,56},{9,1},... | collective-permute-start | bytes 786440 | tf_op jit(solution)/shard_map/ppermute | solution.py:412
  53.2 22.2 %collective-permute-done.4.refs_5_ = f32[2,2,64,256]{3,2,1,0:T(8,128)} collective-permute-done((f32[2,2,64,256]{3,2,1,0:T(8,128)}, f32[2,2,64,256]{3,2,1,0:T(8,128)}, u32[]{:S(2)}, u32[]{:S(2)}) %collective-permute-start.4) | collective-permute-done | bytes 262176 | tf_op jit(solution)/shard_map/ppermute | solution.py:412
  75.5 2.4 collective-permute-done.refs_1_
  77.8 2.4 shard_map.68
  80.3 4.2 %collective-permute-start.7 = (f32[2,4,64,256]{3,2,1,0:T(8,128)}, f32[2,4,64,256]{3,2,1,0:T(8,128)}, u32[]{:S(2)}, u32[]{:S(2)}) collective-permute-start(f32[2,4,64,256]{3,2,1,0:T(8,128)} %get-tuple-element.143), channel_id=1, source_target_pairs={{0,64},{64,128},{128,192},{1,65},{65,129},{129,193},{2,66},{66,130... | collective-permute-start | bytes 1572872 | tf_op jit(solution)/shard_map/ppermute | solution.py:538
  87.9 5.9 %collective-permute-start.9 = (f32[8,4,8,256]{3,2,1,0:T(8,128)}, f32[8,4,8,256]{3,2,1,0:T(8,128)}, u32[]{:S(2)}, u32[]{:S(2)}) collective-permute-start(f32[8,4,8,256]{3,2,1,0:T(8,128)} %get-tuple-element.194), channel_id=1, source_target_pairs={{0,64},{64,128},{128,192},{1,65},{65,129},{129,193},{2,66},{66,130... | collective-permute-start | bytes 786440 | tf_op jit(solution)/shard_map/ppermute | solution.py:539
  96.5 5.0 %collective-permute-done.8.hr_ref = f32[2,4,64,256]{3,2,1,0:T(8,128)} collective-permute-done((f32[2,4,64,256]{3,2,1,0:T(8,128)}, f32[2,4,64,256]{3,2,1,0:T(8,128)}, u32[]{:S(2)}, u32[]{:S(2)}) %collective-permute-start.8) | collective-permute-done | bytes 524320 | tf_op jit(solution)/shard_map/ppermute | solution.py:538
  101.5 3.5 %collective-permute-done.10.sr_ref = f32[8,4,8,256]{3,2,1,0:T(8,128)} collective-permute-done((f32[8,4,8,256]{3,2,1,0:T(8,128)}, f32[8,4,8,256]{3,2,1,0:T(8,128)}, u32[]{:S(2)}, u32[]{:S(2)}) %collective-permute-start.10) | collective-permute-done | bytes 262176 | tf_op jit(solution)/shard_map/ppermute | solution.py:540
  106.9 20.4 %shard_map.71 = (f32[8,2,2,64,256]{4,3,2,1,0:T(8,128)}, f32[8,10,2,128]{3,2,1,0:T(2,128)S(1)}) custom-call(s32[4]{0:T(128)S(1)} %pad_add_fusion.1.where, s32[1280]{0:T(1024)S(1)} %get-tuple-element.196.spots, s32[1280]{0:T(1024)S(1)} %get-tuple-element.195.lanes, f32[2,4,64,256]{3,2,1,0:T(8,128)} %collective-permute-done.7.hl_ref, ...), custom_call_target="tpu_custom_call" | custom-call | flops 33554432 | bytes 8388608 | tf_op jit(solution)/shard_map/pallas_call | solution.py:45
  127.3 13.8 %all_to_all.21.parts = f32[8,10,2,128]{3,2,1,0:T(2,128)S(1)} all-to-all(f32[8,10,2,128]{3,2,1,0:T(2,128)S(1)} %get-tuple-element.146), channel_id=1, replica_groups=mesh['x'=4,'z'=8,'y'=4,'core'=2] {'z'}, dimensions={0} | all-to-all | bytes 163840 | tf_op jit(solution)/shard_map/all_to_all | solution.py:416
  141.4 1.7 collective-permute-start.16
  143.1 2.4 collective-permute-start.15
  145.5 1.9 collective-permute-start.14
  147.6 1.6 collective-permute-start.12
  149.6 6.7 %all-to-all-start.2 = ((f32[16,2,64,256]{3,2,1,0:T(8,128)}), f32[16,2,64,256]{3,2,1,0:T(8,128)}, u32[]{:S(2)}, u32[]{:S(2)}) async-start(f32[16,2,64,256]{3,2,1,0:T(8,128)} %bitcast.17), calls=%async_computation.2 | async-start | bytes 4194304 | tf_op jit(solution)/shard_map/all_to_all | solution.py:416
  156.3 1.6 collective-permute-start.21
  162.5 2.5 collective-permute-start.18
  165.0 39.0 %collective-permute-done.21.refs_1_ = f32[16,2,64,256]{3,2,1,0:T(8,128)} collective-permute-done((f32[16,2,64,256]{3,2,1,0:T(8,128)S(1)}, f32[16,2,64,256]{3,2,1,0:T(8,128)}, u32[]{:S(2)}, u32[]{:S(2)}) %collective-permute-start.21) | collective-permute-done | bytes 2097184 | tf_op jit(solution)/shard_map/ppermute | solution.py:412
  204.0 1.3 slice.80
  206.2 1.9 collective-permute-start.23
  208.1 1.3 slice.81
  210.2 21.1 %collective-permute-done.23.refs_3_ = f32[8,2,64,256]{3,2,1,0:T(8,128)S(1)} collective-permute-done((f32[8,2,64,256]{3,2,1,0:T(8,128)S(1)}, f32[8,2,64,256]{3,2,1,0:T(8,128)S(1)}, u32[]{:S(2)}, u32[]{:S(2)}) %collective-permute-start.23) | collective-permute-done | bytes 1048608 | tf_op jit(solution)/shard_map/ppermute | solution.py:412
  231.2 4.8 %collective-permute-done.24.refs_4_ = f32[8,2,64,256]{3,2,1,0:T(8,128)S(1)} collective-permute-done((f32[8,2,64,256]{3,2,1,0:T(8,128)S(1)}, f32[8,2,64,256]{3,2,1,0:T(8,128)S(1)}, u32[]{:S(2)}, u32[]{:S(2)}) %collective-permute-start.24) | collective-permute-done | bytes 1048608 | tf_op jit(solution)/shard_map/ppermute | solution.py:412
  236.1 2.6 %collective-permute-done.29.refs_9_ = f32[8,2,64,256]{3,2,1,0:T(8,128)S(1)} collective-permute-done((f32[8,2,64,256]{3,2,1,0:T(8,128)S(1)}, f32[8,2,64,256]{3,2,1,0:T(8,128)S(1)}, u32[]{:S(2)}, u32[]{:S(2)}) %collective-permute-start.29) | collective-permute-done | bytes 1048608 | tf_op jit(solution)/shard_map/ppermute | solution.py:465
  238.7 17.0 %shard_map.74 = f32[16,2,64,256]{3,2,1,0:T(8,128)} custom-call(s32[4]{0:T(128)S(1)} %pad_add_fusion.1.where, f32[136,128]{1,0:T(8,128)S(1)} %get-tuple-element.149.g0, f32[136,128]{1,0:T(8,128)S(1)} %collective-permute-done.18.g1, f32[136,128]{1,0:T(8,128)S(1)} %collective-permute-done.19.g2, f32[136,128]{1,0:T(8,128)S(1)} %collective-permute-done.20.g3, ...), custom_call_target="tpu_custom_call" | custom-call | flops 134217728 | bytes 16777216 | tf_op jit(solution)/shard_map/pallas_call | solution.py:45
  255.8 3.1 %copy.14 = f32[16,2,64,256]{3,2,1,0:T(8,128)} copy(f32[16,2,64,256]{3,2,1,0:T(8,128)} %all-to-all-done.2) | data formatting | bytes 4194304
  (78 shorter events, 20.3 us)
Async XLA Ops:
  17.8 68.0 %all-to-all-start.1 = ((f32[8,16,8,256]{3,2,1,0:T(8,128)}), f32[8,16,8,256]{3,2,1,0:T(8,128)S(1)}, u32[]{:S(2)}, u32[]{:S(2)}) async-start(f32[8,16,8,256]{3,2,1,0:T(8,128)} %copy-done.1), calls=%async_computation.1 | async-start | bytes 2097152 | tf_op jit(solution)/shard_map/all_to_all | solution.py:416
  23.6 17.9 %collective-permute-start.6 = (f32[2,2,64,256]{3,2,1,0:T(8,128)}, f32[2,2,64,256]{3,2,1,0:T(8,128)}, u32[]{:S(2)}, u32[]{:S(2)}) collective-permute-start(f32[2,2,64,256]{3,2,1,0:T(8,128)} %get-tuple-element.185), channel_id=1, source_target_pairs={{56,0},{0,8},{8,16},{16,24},{24,32},{32,40},{40,48},{48,56},{57,1}... | collective-permute-start | bytes 786440 | tf_op jit(solution)/shard_map/ppermute | solution.py:412
  24.6 18.4 %collective-permute-start.5 = (f32[2,2,64,256]{3,2,1,0:T(8,128)}, f32[2,2,64,256]{3,2,1,0:T(8,128)}, u32[]{:S(2)}, u32[]{:S(2)}) collective-permute-start(f32[2,2,64,256]{3,2,1,0:T(8,128)} %get-tuple-element.186), channel_id=1, source_target_pairs={{48,0},{56,8},{0,16},{8,24},{16,32},{24,40},{32,48},{40,56},{49,1}... | collective-permute-start | bytes 786440 | tf_op jit(solution)/shard_map/ppermute | solution.py:412
  25.9 49.5 %collective-permute-start.4 = (f32[2,2,64,256]{3,2,1,0:T(8,128)}, f32[2,2,64,256]{3,2,1,0:T(8,128)}, u32[]{:S(2)}, u32[]{:S(2)}) collective-permute-start(f32[2,2,64,256]{3,2,1,0:T(8,128)} %get-tuple-element.187), channel_id=1, source_target_pairs={{40,0},{48,8},{56,16},{0,24},{8,32},{16,40},{24,48},{32,56},{41,1}... | collective-permute-start | bytes 786440 | tf_op jit(solution)/shard_map/ppermute | solution.py:412
  30.6 44.9 %collective-permute-start.3 = (f32[2,2,64,256]{3,2,1,0:T(8,128)}, f32[2,2,64,256]{3,2,1,0:T(8,128)}, u32[]{:S(2)}, u32[]{:S(2)}) collective-permute-start(f32[2,2,64,256]{3,2,1,0:T(8,128)} %get-tuple-element.188), channel_id=1, source_target_pairs={{32,0},{40,8},{48,16},{56,24},{0,32},{8,40},{16,48},{24,56},{33,1}... | collective-permute-start | bytes 786440 | tf_op jit(solution)/shard_map/ppermute | solution.py:412
  31.1 44.3 %collective-permute-start.2 = (f32[2,2,64,256]{3,2,1,0:T(8,128)}, f32[2,2,64,256]{3,2,1,0:T(8,128)}, u32[]{:S(2)}, u32[]{:S(2)}) collective-permute-start(f32[2,2,64,256]{3,2,1,0:T(8,128)} %get-tuple-element.189), channel_id=1, source_target_pairs={{24,0},{32,8},{40,16},{48,24},{56,32},{0,40},{8,48},{16,56},{25,1}... | collective-permute-start | bytes 786440 | tf_op jit(solution)/shard_map/ppermute | solution.py:412
  41.4 34.0 %collective-permute-start.1 = (f32[2,2,64,256]{3,2,1,0:T(8,128)}, f32[2,2,64,256]{3,2,1,0:T(8,128)S(1)}, u32[]{:S(2)}, u32[]{:S(2)}) collective-permute-start(f32[2,2,64,256]{3,2,1,0:T(8,128)} %get-tuple-element.190), channel_id=1, source_target_pairs={{16,0},{24,8},{32,16},{40,24},{48,32},{56,40},{0,48},{8,56},{17,1}... | collective-permute-start | bytes 786440 | tf_op jit(solution)/shard_map/ppermute | solution.py:412
  43.0 34.8 %collective-permute-start = (f32[2,2,64,256]{3,2,1,0:T(8,128)}, f32[2,2,64,256]{3,2,1,0:T(8,128)S(1)}, u32[]{:S(2)}, u32[]{:S(2)}) collective-permute-start(f32[2,2,64,256]{3,2,1,0:T(8,128)} %get-tuple-element.191), channel_id=1, source_target_pairs={{8,0},{16,8},{24,16},{32,24},{40,32},{48,40},{56,48},{0,56},{9,1},... | collective-permute-start | bytes 786440 | tf_op jit(solution)/shard_map/ppermute | solution.py:412
  80.3 16.2 %collective-permute-start.7 = (f32[2,4,64,256]{3,2,1,0:T(8,128)}, f32[2,4,64,256]{3,2,1,0:T(8,128)}, u32[]{:S(2)}, u32[]{:S(2)}) collective-permute-start(f32[2,4,64,256]{3,2,1,0:T(8,128)} %get-tuple-element.143), channel_id=1, source_target_pairs={{0,64},{64,128},{128,192},{1,65},{65,129},{129,193},{2,66},{66,130... | collective-permute-start | bytes 1572872 | tf_op jit(solution)/shard_map/ppermute | solution.py:538
  84.5 17.0 %collective-permute-start.8 = (f32[2,4,64,256]{3,2,1,0:T(8,128)}, f32[2,4,64,256]{3,2,1,0:T(8,128)}, u32[]{:S(2)}, u32[]{:S(2)}) collective-permute-start(f32[2,4,64,256]{3,2,1,0:T(8,128)} %get-tuple-element.144), channel_id=1, source_target_pairs={{64,0},{128,64},{192,128},{65,1},{129,65},{193,129},{66,2},{130,66... | collective-permute-start | bytes 1572872 | tf_op jit(solution)/shard_map/ppermute | solution.py:538
  86.6 18.4 %collective-permute-start.10 = (f32[8,4,8,256]{3,2,1,0:T(8,128)}, f32[8,4,8,256]{3,2,1,0:T(8,128)}, u32[]{:S(2)}, u32[]{:S(2)}) collective-permute-start(f32[8,4,8,256]{3,2,1,0:T(8,128)} %get-tuple-element.193), channel_id=1, source_target_pairs={{64,0},{128,64},{192,128},{65,1},{129,65},{193,129},{66,2},{130,66... | collective-permute-start | bytes 786440 | tf_op jit(solution)/shard_map/ppermute | solution.py:540
  87.9 17.1 %collective-permute-start.9 = (f32[8,4,8,256]{3,2,1,0:T(8,128)}, f32[8,4,8,256]{3,2,1,0:T(8,128)}, u32[]{:S(2)}, u32[]{:S(2)}) collective-permute-start(f32[8,4,8,256]{3,2,1,0:T(8,128)} %get-tuple-element.194), channel_id=1, source_target_pairs={{0,64},{64,128},{128,192},{1,65},{65,129},{129,193},{2,66},{66,130... | collective-permute-start | bytes 786440 | tf_op jit(solution)/shard_map/ppermute | solution.py:539
  141.1 6.6 %collective-permute-start.17 = (f32[10,16,128]{2,1,0:T(8,128)S(1)}, f32[10,16,128]{2,1,0:T(8,128)S(1)}, u32[]{:S(2)}, u32[]{:S(2)}) collective-permute-start(f32[10,16,128]{2,1,0:T(8,128)S(1)} %shard_map.72.refs_0_), channel_id=1, source_target_pairs={{7,0},{6,1},{1,2},{0,3},{3,4},{2,5},{5,6},{4,7},{15,8},{14,9},{9,1... | collective-permute-start | bytes 245768 | tf_op jit(solution)/shard_map/ppermute | solution.py:452
  141.4 7.9 %collective-permute-start.16 = (f32[10,16,128]{2,1,0:T(8,128)S(1)}, f32[10,16,128]{2,1,0:T(8,128)S(1)}, u32[]{:S(2)}, u32[]{:S(2)}) collective-permute-start(f32[10,16,128]{2,1,0:T(8,128)S(1)} %shard_map.72.refs_0_), channel_id=1, source_target_pairs={{6,0},{7,1},{0,2},{1,3},{2,4},{3,5},{4,6},{5,7},{14,8},{15,9},{8,1... | collective-permute-start | bytes 245768 | tf_op jit(solution)/shard_map/ppermute | solution.py:452
  143.1 13.2 %collective-permute-start.15 = (f32[10,16,128]{2,1,0:T(8,128)S(1)}, f32[10,16,128]{2,1,0:T(8,128)S(1)}, u32[]{:S(2)}, u32[]{:S(2)}) collective-permute-start(f32[10,16,128]{2,1,0:T(8,128)S(1)} %shard_map.72.refs_0_), channel_id=1, source_target_pairs={{5,0},{4,1},{7,2},{6,3},{1,4},{0,5},{3,6},{2,7},{13,8},{12,9},{15,... | collective-permute-start | bytes 245768 | tf_op jit(solution)/shard_map/ppermute | solution.py:452
  145.5 12.4 %collective-permute-start.14 = (f32[10,16,128]{2,1,0:T(8,128)S(1)}, f32[10,16,128]{2,1,0:T(8,128)S(1)}, u32[]{:S(2)}, u32[]{:S(2)}) collective-permute-start(f32[10,16,128]{2,1,0:T(8,128)S(1)} %shard_map.72.refs_0_), channel_id=1, source_target_pairs={{4,0},{5,1},{6,2},{7,3},{0,4},{1,5},{2,6},{3,7},{12,8},{13,9},{14,... | collective-permute-start | bytes 245768 | tf_op jit(solution)/shard_map/ppermute | solution.py:452
  147.4 10.9 %collective-permute-start.13 = (f32[10,16,128]{2,1,0:T(8,128)S(1)}, f32[10,16,128]{2,1,0:T(8,128)S(1)}, u32[]{:S(2)}, u32[]{:S(2)}) collective-permute-start(f32[10,16,128]{2,1,0:T(8,128)S(1)} %shard_map.72.refs_0_), channel_id=1, source_target_pairs={{3,0},{2,1},{5,2},{4,3},{7,4},{6,5},{1,6},{0,7},{11,8},{10,9},{13,... | collective-permute-start | bytes 245768 | tf_op jit(solution)/shard_map/ppermute | solution.py:452
  147.6 10.7 %collective-permute-start.12 = (f32[10,16,128]{2,1,0:T(8,128)S(1)}, f32[10,16,128]{2,1,0:T(8,128)S(1)}, u32[]{:S(2)}, u32[]{:S(2)}) collective-permute-start(f32[10,16,128]{2,1,0:T(8,128)S(1)} %shard_map.72.refs_0_), channel_id=1, source_target_pairs={{2,0},{3,1},{4,2},{5,3},{6,4},{7,5},{0,6},{1,7},{10,8},{11,9},{12,... | collective-permute-start | bytes 245768 | tf_op jit(solution)/shard_map/ppermute | solution.py:452
  149.3 9.0 %collective-permute-start.11 = (f32[10,16,128]{2,1,0:T(8,128)S(1)}, f32[10,16,128]{2,1,0:T(8,128)S(1)}, u32[]{:S(2)}, u32[]{:S(2)}) collective-permute-start(f32[10,16,128]{2,1,0:T(8,128)S(1)} %shard_map.72.refs_0_), channel_id=1, source_target_pairs={{1,0},{0,1},{3,2},{2,3},{5,4},{4,5},{7,6},{6,7},{9,8},{8,9},{11,10... | collective-permute-start | bytes 245768 | tf_op jit(solution)/shard_map/ppermute | solution.py:452
  149.6 106.2 %all-to-all-start.2 = ((f32[16,2,64,256]{3,2,1,0:T(8,128)}), f32[16,2,64,256]{3,2,1,0:T(8,128)}, u32[]{:S(2)}, u32[]{:S(2)}) async-start(f32[16,2,64,256]{3,2,1,0:T(8,128)} %bitcast.17), calls=%async_computation.2 | async-start | bytes 4194304 | tf_op jit(solution)/shard_map/all_to_all | solution.py:416
  156.3 47.7 %collective-permute-start.21 = (f32[16,2,64,256]{3,2,1,0:T(8,128)S(1)}, f32[16,2,64,256]{3,2,1,0:T(8,128)}, u32[]{:S(2)}, u32[]{:S(2)}) collective-permute-start(f32[16,2,64,256]{3,2,1,0:T(8,128)S(1)} %copy-done), channel_id=1, source_target_pairs={{2,0},{4,2},{6,4},{0,6},{3,1},{5,3},{7,5},{1,7},{10,8},{12,10},{14... | collective-permute-start | bytes 6291464 | tf_op jit(solution)/shard_map/ppermute | solution.py:412
  157.9 48.3 %collective-permute-start.22 = (f32[16,2,64,256]{3,2,1,0:T(8,128)S(1)}, f32[16,2,64,256]{3,2,1,0:T(8,128)}, u32[]{:S(2)}, u32[]{:S(2)}) collective-permute-start(f32[16,2,64,256]{3,2,1,0:T(8,128)S(1)} %copy-done), channel_id=1, source_target_pairs={{6,0},{0,2},{2,4},{4,6},{7,1},{1,3},{3,5},{5,7},{14,8},{8,10},{10,... | collective-permute-start | bytes 6291464 | tf_op jit(solution)/shard_map/ppermute | solution.py:412
  160.3 49.1 %collective-permute-start.20 = (f32[136,128]{1,0:T(8,128)S(1)}, f32[136,128]{1,0:T(8,128)S(1)}, u32[]{:S(2)}, u32[]{:S(2)}) collective-permute-start(f32[136,128]{1,0:T(8,128)S(1)} %get-tuple-element.149.g0), channel_id=1, source_target_pairs={{192,0},{0,64},{64,128},{128,192},{193,1},{1,65},{65,129},{129,193... | collective-permute-start | bytes 208904 | tf_op jit(solution)/shard_map/ppermute | solution.py:412
  161.4 48.2 %collective-permute-start.19 = (f32[136,128]{1,0:T(8,128)S(1)}, f32[136,128]{1,0:T(8,128)S(1)}, u32[]{:S(2)}, u32[]{:S(2)}) collective-permute-start(f32[136,128]{1,0:T(8,128)S(1)} %get-tuple-element.149.g0), channel_id=1, source_target_pairs={{128,0},{192,64},{0,128},{64,192},{129,1},{193,65},{1,129},{65,193... | collective-permute-start | bytes 208904 | tf_op jit(solution)/shard_map/ppermute | solution.py:412
  162.5 47.4 %collective-permute-start.18 = (f32[136,128]{1,0:T(8,128)S(1)}, f32[136,128]{1,0:T(8,128)S(1)}, u32[]{:S(2)}, u32[]{:S(2)}) collective-permute-start(f32[136,128]{1,0:T(8,128)S(1)} %get-tuple-element.149.g0), channel_id=1, source_target_pairs={{64,0},{128,64},{192,128},{0,192},{65,1},{129,65},{193,129},{1,193... | collective-permute-start | bytes 208904 | tf_op jit(solution)/shard_map/ppermute | solution.py:412
  204.0 32.0 %collective-permute-start.25 = (f32[16,2,64,256]{3,2,1,0:T(8,128)S(1)}, f32[16,2,64,256]{3,2,1,0:T(8,128)S(1)}, u32[]{:S(2)}, u32[]{:S(2)}) collective-permute-start(f32[16,2,64,256]{3,2,1,0:T(8,128)S(1)} %copy-done), channel_id=1, source_target_pairs={{0,1},{1,0},{2,3},{3,2},{4,5},{5,4},{6,7},{7,6},{8,9},{9,8},{10,11... | collective-permute-start | bytes 6291464 | tf_op jit(solution)/shard_map/ppermute | solution.py:465
  206.2 25.0 %collective-permute-start.23 = (f32[8,2,64,256]{3,2,1,0:T(8,128)S(1)}, f32[8,2,64,256]{3,2,1,0:T(8,128)S(1)}, u32[]{:S(2)}, u32[]{:S(2)}) collective-permute-start(f32[8,2,64,256]{3,2,1,0:T(8,128)S(1)} %slice.80), channel_id=1, source_target_pairs={{2,0},{4,2},{6,4},{0,6},{3,1},{5,3},{7,5},{1,7},{10,8},{12,10},{14... | collective-permute-start | bytes 3145736 | tf_op jit(solution)/shard_map/ppermute | solution.py:412
  209.5 26.6 %collective-permute-start.24 = (f32[8,2,64,256]{3,2,1,0:T(8,128)S(1)}, f32[8,2,64,256]{3,2,1,0:T(8,128)S(1)}, u32[]{:S(2)}, u32[]{:S(2)}) collective-permute-start(f32[8,2,64,256]{3,2,1,0:T(8,128)S(1)} %slice.81), channel_id=1, source_target_pairs={{6,0},{0,2},{2,4},{4,6},{7,1},{1,3},{3,5},{5,7},{14,8},{8,10},{10,... | collective-permute-start | bytes 3145736 | tf_op jit(solution)/shard_map/ppermute | solution.py:412
  209.7 26.4 %collective-permute-start.26 = (f32[16,2,64,256]{3,2,1,0:T(8,128)}, f32[16,2,64,256]{3,2,1,0:T(8,128)S(1)}, u32[]{:S(2)}, u32[]{:S(2)}) collective-permute-start(f32[16,2,64,256]{3,2,1,0:T(8,128)} %collective-permute-done.21.refs_1_), channel_id=1, source_target_pairs={{0,1},{1,0},{2,3},{3,2},{4,5},{5,4},{6,7},{7,6},{8,9},{9,8},{10,11... | collective-permute-start | bytes 6291464 | tf_op jit(solution)/shard_map/ppermute | solution.py:465
  209.9 28.8 %collective-permute-start.27 = (f32[16,2,64,256]{3,2,1,0:T(8,128)}, f32[16,2,64,256]{3,2,1,0:T(8,128)S(1)}, u32[]{:S(2)}, u32[]{:S(2)}) collective-permute-start(f32[16,2,64,256]{3,2,1,0:T(8,128)} %collective-permute-done.22.refs_2_), channel_id=1, source_target_pairs={{0,1},{1,0},{2,3},{3,2},{4,5},{5,4},{6,7},{7,6},{8,9},{9,8},{10,11... | collective-permute-start | bytes 6291464 | tf_op jit(solution)/shard_map/ppermute | solution.py:465
  231.2 4.8 %collective-permute-start.28 = (f32[8,2,64,256]{3,2,1,0:T(8,128)S(1)}, f32[8,2,64,256]{3,2,1,0:T(8,128)S(1)}, u32[]{:S(2)}, u32[]{:S(2)}) collective-permute-start(f32[8,2,64,256]{3,2,1,0:T(8,128)S(1)} %collective-permute-done.23.refs_3_), channel_id=1, source_target_pairs={{0,1},{1,0},{2,3},{3,2},{4,5},{5,4},{6,7},{7,6},{8,9},{9,8},{10,11... | collective-permute-start | bytes 3145736 | tf_op jit(solution)/shard_map/ppermute | solution.py:465
  236.0 2.7 %collective-permute-start.29 = (f32[8,2,64,256]{3,2,1,0:T(8,128)S(1)}, f32[8,2,64,256]{3,2,1,0:T(8,128)S(1)}, u32[]{:S(2)}, u32[]{:S(2)}) collective-permute-start(f32[8,2,64,256]{3,2,1,0:T(8,128)S(1)} %collective-permute-done.24.refs_4_), channel_id=1, source_target_pairs={{0,1},{1,0},{2,3},{3,2},{4,5},{5,4},{6,7},{7,6},{8,9},{9,8},{10,11... | collective-permute-start | bytes 3145736 | tf_op jit(solution)/shard_map/ppermute | solution.py:465
  (10 other events, 80.7 us)

commit v3 on v2

--- a/solution.py
+++ b/solution.py
@@ -38,7 +38,7 @@
     return jax.ShapeDtypeStruct(dims, F32)
 
 
-LIMITS = {"ends": 8, "sweeps": 32, "analysis": 32, "more": 16}
+LIMITS = {"ends": 8, "sweeps": 63, "analysis": 32, "more": 16}
 
 
 def call(kernel, outs, ins, specs, out_specs, scratch, flops, moved, name):
@@ -116,9 +116,9 @@
     @pl.loop(0, groups)
     def _(c):
         j = first + c * GROUP
+        lane_sums(q, j + GROUP, band, sums)
         for k in range(GROUP):
             step(j + k)
-        lane_sums(q, j + GROUP, band, sums)
 
 
 def gather_all(where, spots, lanes, press, found, copies):
@@ -146,22 +146,18 @@
         copies[copy] = out[...]
 
 
-def sweeps_kernel(where, spots, lanes, hl_ref, hr_ref, s_mid, sl_ref, sr_ref, *refs):
+def sweeps_kernel(where, spots, lanes, hl_ref, hr_ref, sources, *refs):
     parts, refs = refs[:NZ], refs[NZ:]
     out, pred_ref, h_all, raw, s_ref, qs, qw, qb, qc, rest, weight, sums, band, *refs = refs
-    press, found, sems, in_sems, h_sems, s_sems = refs
-    cuts = [(0, HALO), (HALO, DEPTH), (HALO + DEPTH, HALO)]
+    press, found, sems, in_sems, h_sems, s_sem = refs
 
     halos = []
     for n, source in enumerate((hl_ref, hr_ref)):
-        there = h_all.at[:, pl.ds(1 + cuts[2 * n][0], HALO)]
+        there = h_all.at[:, pl.ds(1 + n * (HALO + DEPTH), HALO)]
         halos.append(pltpu.make_async_copy(source, there, h_sems.at[n]))
     arrivals = [pltpu.make_async_copy(parts[d], raw.at[d], in_sems.at[d]) for d in range(NZ)]
 
-    strips = []
-    for n, source in enumerate((sl_ref, s_mid, sr_ref)):
-        there = s_ref.at[:, pl.ds(*cuts[n])]
-        strips.append(pltpu.make_async_copy(source, there, s_sems.at[n]))
+    strips = [pltpu.make_async_copy(sources, s_ref.at[:, pl.ds(0, FULL)], s_sem)]
     for copy in [*arrivals, *halos, *strips]:
         copy.start()
 
@@ -374,14 +370,14 @@
         sweeps_kernel,
         [PARTS, PRED],
         ins,
-        [SM] * 3 + [ANY] * (5 + NZ),
+        [SM] * 3 + [ANY] * (3 + NZ),
         [HBM, VM],
         [pltpu.VMEM((SUB, ROOM, NY, NW), F32), pltpu.VMEM((NZ, SUB, LAY, NY, NW), F32)]
         + [pltpu.VMEM((NMEM, FULL + 2, ROWS_OF, NW), F32)]
         + [pltpu.VMEM((ROOM, NY, NW), F32)] * 7
         + [pltpu.VMEM((NW, NW), jnp.bfloat16), PRESSED, FOUND]
         + [pltpu.SemaphoreType.DMA((SUB, HALVES, NZ))]
-        + [pltpu.SemaphoreType.DMA((n,)) for n in (NZ, 2, 3)],
+        + [pltpu.SemaphoreType.DMA((NZ,)), pltpu.SemaphoreType.DMA((2,)), pltpu.SemaphoreType.DMA],
         64 * BIG,
         16 * BIG,
         "sweeps",
@@ -427,10 +423,13 @@
         copy.wait()
 
 
-def strips_kernel(strips, out):
+def strips_kernel(left, strips, right, out):
+    parts = [left[n] for n in range(HALO // LAY)]
+    parts += [strips[n] for n in range(NZ)]
+    parts += [right[n] for n in range(HALO // LAY)]
     for copy in range(NMEM):
-        for slab in range(NZ):
-            out[copy, LAY * slab : LAY * slab + LAY] = strips[slab]
+        for n, part in enumerate(parts):
+            out[copy, LAY * n : LAY * n + LAY] = part
 
 
 def preds_kernel(parts, out):
@@ -451,11 +450,6 @@
         pairs = [(group_at(i, e), i) for i in range(NMEM)]
         parts.append(lax.ppermute(array, ("y", "core"), pairs))
     return parts
-
-
-def to_mem(kernel, parts, dims, name):
-    copies = call(kernel, shape(NMEM, *dims), [parts], [VM], VM, [], 2**20, 2**20, name)
-    return exchange(copies, ("y", "core"))
 
 
 def body(logperm, source, obs_cells, obs_values, obs_prec):
@@ -483,6 +477,10 @@
         "strip",
     )
     strips = exchange(strip, "z")
+    up = [(i, i + 1) for i in range(NX - 1)]
+    down = [(i + 1, i) for i in range(NX - 1)]
+    s_left = lax.ppermute(strips[NZ - HALO // LAY :], "x", up)
+    s_right = lax.ppermute(strips[: HALO // LAY], "x", down)
 
     def members_of(group):
         start = ((group & (NZ - 1)) * SUB, 0, 0, 0)
@@ -492,7 +490,18 @@
     parts = [members_of(z)] + [None] * (NZ - 1)
     for d in (4, 1, 7, 2, 6, 3, 5):
         parts[d] = shift_from(members_of(z - d), "z", NZ, d)
-    sources = to_mem(strips_kernel, strips, (DEPTH, ROWS_OF, NW), "strips")
+    copies = call(
+        strips_kernel,
+        shape(NMEM, FULL, ROWS_OF, NW),
+        [s_left, strips, s_right],
+        [VM] * 3,
+        VM,
+        [],
+        2**20,
+        2**20,
+        "strips",
+    )
+    sources = exchange(copies, ("y", "core"))
 
     cells, prec, values = lax.sort((obs_cells, obs_prec, obs_values), num_keys=1)
     block = lax.shift_right_logical(cells, BLOCK_BITS)
@@ -533,14 +542,9 @@
         4 * BIG,
         "ends",
     )
-    up = [(i, i + 1) for i in range(NX - 1)]
-    down = [(i + 1, i) for i in range(NX - 1)]
     h_left, h_right = lax.ppermute(last, "x", up), lax.ppermute(first, "x", down)
-    s_left = lax.ppermute(sources[:, DEPTH - HALO :], "x", up)
-    s_right = lax.ppermute(sources[:, :HALO], "x", down)
-
     sent, pred = sweep(
-        where, spots_0, lanes_0, h_left, h_right, sources, s_left, s_right, *parts
+        where, spots_0, lanes_0, h_left, h_right, sources, *parts
     )
 
     def group_preds(parts):

time: 262 us -> 262 us (level)
  starting transfers between devices: 65 us -> 70.7 us
  waiting for transfers between devices: 102 us -> 97.3 us
    ppermute x14, starting transfers between devices: 32.3 us -> 39.1 us  [shift_from(): lax.ppermute(array, axis, [((i + by) % size, i) for i in range(size)])]
    ppermute x14, waiting for transfers between devices: 90.4 us -> 83.9 us  [shift_from(): lax.ppermute(array, axis, [((i + by) % size, i) for i in range(size)])]
    ppermute x1, waiting for transfers between devices: 0.01 us -> 5.02 us  [body(): lax.ppermute(last, 'x', up)]
    unnamed x21 -> x37, local copies, waits for them, and re-layouts: 7.07 us -> 6.73 us
  transfers between devices with their start and end apart: 32 -> 32, of which waited for: 9 -> 10; matrix products, arithmetic and copies ran while one was open for 5% -> 5% of each run, Pallas kernels for 8% -> 7%
where the time goes in v3:
time: 262 us; the launch traced here: 259 us
  waiting for transfers between devices  97.3 us (37%)
  starting transfers between devices  70.7 us (27%)
  Pallas kernels  40.4 us (15%)
  blocking collectives  28.5 us (11%)
  local copies, waits for them, and re-layouts  10.6 us (4%)
  other arithmetic  8.13 us (3%)
  between operations  2.85 us (1%)
    ppermute x14, waiting for transfers between devices, shift_from(): lax.ppermute(array, axis, [((i + by) % size, i) for i in range(size)])  83.9 us
    pallas_call x7, Pallas kernels, call(): pl.pallas_call(kernel, out_shape=outs, in_specs=specs, out_specs=out_spec...  40.4 us
    ppermute x14, starting transfers between devices, shift_from(): lax.ppermute(array, axis, [((i + by) % size, i) for i in range(size)])  39.1 us
    all_to_all x2, blocking collectives, exchange(): return lax.all_to_all(copies, axis, 0, 0, tiled=True)  28.5 us
    all_to_all x2, starting transfers between devices, exchange(): return lax.all_to_all(copies, axis, 0, 0, tiled=True)  11.3 us
    ppermute x7, starting transfers between devices, round_mem(): parts.append(lax.ppermute(array, ('y', 'core'), pairs))  8.32 us
    unnamed x37, local copies, waits for them, and re-layouts  6.73 us
    sort x1, other arithmetic, body(): lax.sort((obs_cells, obs_prec, obs_values), num_keys=1)  5.95 us
  transfers between devices with their start and end apart: 32, of which 10 were waited for; matrix products, arithmetic and copies ran while one was open for 5% of the time, Pallas kernels for 7%

profile of v3, /device:TPU:64, one launch (start us, length us, event | category | flops | bytes accessed | tf_op | source)
XLA Modules:
  0.0 259.2 jit_solution(14168712585771139139)
XLA Ops:
  2.3 14.3 %all_to_all.20.strips = f32[8,2,8,256]{3,2,1,0:T(8,128)S(1)} all-to-all(f32[8,2,8,256]{3,2,1,0:T(8,128)} %shard_map.69), channel_id=1, replica_groups=mesh['x'=4,'z'=8,'y'=4,'core'=2] {'z'}, dimensions={0} | all-to-all | bytes 262144 | tf_op jit(solution)/shard_map/all_to_all | solution.py:412
  17.9 4.7 %collective-permute-start.9 = (f32[2,2,8,256]{3,2,1,0:T(8,128)S(1)}, f32[2,2,8,256]{3,2,1,0:T(8,128)S(1)}, u32[]{:S(2)}, u32[]{:S(2)}) collective-permute-start(f32[2,2,8,256]{3,2,1,0:T(8,128)S(1)} %get-tuple-element.194), channel_id=1, source_target_pairs={{0,64},{64,128},{128,192},{1,65},{65,129},{129,193},{2,66},{66,130... | collective-permute-start | bytes 98312 | tf_op jit(solution)/shard_map/ppermute | solution.py:482
  22.6 1.6 collective-permute-done.9.left
  25.4 4.5 %all-to-all-start.1 = ((f32[8,24,8,256]{3,2,1,0:T(8,128)}), f32[8,24,8,256]{3,2,1,0:T(8,128)}, u32[]{:S(2)}, u32[]{:S(2)}) async-start(f32[8,24,8,256]{3,2,1,0:T(8,128)} %copy-done.2), calls=%async_computation.1 | async-start | bytes 3145728 | tf_op jit(solution)/shard_map/all_to_all | solution.py:412
  33.4 4.6 %collective-permute-start.4 = (f32[2,2,64,256]{3,2,1,0:T(8,128)}, f32[2,2,64,256]{3,2,1,0:T(8,128)S(1)}, u32[]{:S(2)}, u32[]{:S(2)}) collective-permute-start(f32[2,2,64,256]{3,2,1,0:T(8,128)} %get-tuple-element.187), channel_id=1, source_target_pairs={{40,0},{48,8},{56,16},{0,24},{8,32},{16,40},{24,48},{32,56},{41,1}... | collective-permute-start | bytes 786440 | tf_op jit(solution)/shard_map/ppermute | solution.py:408
  38.6 4.3 %collective-permute-start.2 = (f32[2,2,64,256]{3,2,1,0:T(8,128)}, f32[2,2,64,256]{3,2,1,0:T(8,128)S(1)}, u32[]{:S(2)}, u32[]{:S(2)}) collective-permute-start(f32[2,2,64,256]{3,2,1,0:T(8,128)} %get-tuple-element.189), channel_id=1, source_target_pairs={{24,0},{32,8},{40,16},{48,24},{56,32},{0,40},{8,48},{16,56},{25,1}... | collective-permute-start | bytes 786440 | tf_op jit(solution)/shard_map/ppermute | solution.py:408
  42.9 7.2 %collective-permute-start.1 = (f32[2,2,64,256]{3,2,1,0:T(8,128)}, f32[2,2,64,256]{3,2,1,0:T(8,128)S(1)}, u32[]{:S(2)}, u32[]{:S(2)}) collective-permute-start(f32[2,2,64,256]{3,2,1,0:T(8,128)} %get-tuple-element.190), channel_id=1, source_target_pairs={{16,0},{24,8},{32,16},{40,24},{48,32},{56,40},{0,48},{8,56},{17,1}... | collective-permute-start | bytes 786440 | tf_op jit(solution)/shard_map/ppermute | solution.py:408
  50.1 10.1 %collective-permute-start = (f32[2,2,64,256]{3,2,1,0:T(8,128)}, f32[2,2,64,256]{3,2,1,0:T(8,128)S(1)}, u32[]{:S(2)}, u32[]{:S(2)}) collective-permute-start(f32[2,2,64,256]{3,2,1,0:T(8,128)} %get-tuple-element.191), channel_id=1, source_target_pairs={{8,0},{16,8},{24,16},{32,24},{40,32},{48,40},{56,48},{0,56},{9,1},... | collective-permute-start | bytes 786440 | tf_op jit(solution)/shard_map/ppermute | solution.py:408
  60.2 5.9 %sort.31 = (s32[4096]{0:T(1024)S(1)}, f32[4096]{0:T(1024)S(1)}, f32[4096]{0:T(1024)S(1)}, s32[4096]{0:T(1024)}) sort(s32[4096]{0:T(1024)S(1)} %copy-done.15, f32[4096]{0:T(1024)S(1)} %copy-done.16, f32[4096]{0:T(1024)S(1)} %copy-done.17, s32[4096]{0:T(1024)S(1)} %iota.26), dimensions={0}, to_apply=%region_0.0 | sort | flops 49152 | bytes 131072 | tf_op jit(solution)/shard_map/sort | solution.py:506
  66.2 16.4 %collective-permute-done.4.refs_5_ = f32[2,2,64,256]{3,2,1,0:T(8,128)S(1)} collective-permute-done((f32[2,2,64,256]{3,2,1,0:T(8,128)}, f32[2,2,64,256]{3,2,1,0:T(8,128)S(1)}, u32[]{:S(2)}, u32[]{:S(2)}) %collective-permute-start.4) | collective-permute-done | bytes 262176 | tf_op jit(solution)/shard_map/ppermute | solution.py:408
  82.6 2.7 %collective-permute-done.refs_1_ = f32[2,2,64,256]{3,2,1,0:T(8,128)S(1)} collective-permute-done((f32[2,2,64,256]{3,2,1,0:T(8,128)}, f32[2,2,64,256]{3,2,1,0:T(8,128)S(1)}, u32[]{:S(2)}, u32[]{:S(2)}) %collective-permute-start) | collective-permute-done | bytes 262176 | tf_op jit(solution)/shard_map/ppermute | solution.py:408
  86.4 4.2 %collective-permute-start.7 = (f32[2,4,64,256]{3,2,1,0:T(8,128)S(1)}, f32[2,4,64,256]{3,2,1,0:T(8,128)S(1)}, u32[]{:S(2)}, u32[]{:S(2)}) collective-permute-start(f32[2,4,64,256]{3,2,1,0:T(8,128)S(1)} %get-tuple-element.143), channel_id=1, source_target_pairs={{0,64},{64,128},{128,192},{1,65},{65,129},{129,193},{2,66},{66,130... | collective-permute-start | bytes 1572872 | tf_op jit(solution)/shard_map/ppermute | solution.py:545
  96.0 5.0 %collective-permute-done.7.hl_ref = f32[2,4,64,256]{3,2,1,0:T(8,128)S(1)} collective-permute-done((f32[2,4,64,256]{3,2,1,0:T(8,128)S(1)}, f32[2,4,64,256]{3,2,1,0:T(8,128)S(1)}, u32[]{:S(2)}, u32[]{:S(2)}) %collective-permute-start.7) | collective-permute-done | bytes 524320 | tf_op jit(solution)/shard_map/ppermute | solution.py:545
  101.0 4.2 %collective-permute-done.8.hr_ref = f32[2,4,64,256]{3,2,1,0:T(8,128)S(1)} collective-permute-done((f32[2,4,64,256]{3,2,1,0:T(8,128)S(1)}, f32[2,4,64,256]{3,2,1,0:T(8,128)S(1)}, u32[]{:S(2)}, u32[]{:S(2)}) %collective-permute-start.8) | collective-permute-done | bytes 524320 | tf_op jit(solution)/shard_map/ppermute | solution.py:545
  106.0 21.1 %shard_map.71 = (f32[8,2,2,64,256]{4,3,2,1,0:T(8,128)}, f32[8,10,2,128]{3,2,1,0:T(2,128)}) custom-call(s32[4]{0:T(128)} %pad_add_fusion.1.where, s32[1280]{0:T(1024)} %get-tuple-element.196.spots, s32[1280]{0:T(1024)} %get-tuple-element.195.lanes, f32[2,4,64,256]{3,2,1,0:T(8,128)} %copy-done.13, f32[2,4,64,256]{3,2,1,0:T(8,128)} %copy-done.14, ...), custom_call_target="tpu_custom_call" | custom-call | flops 33554432 | bytes 8388608 | tf_op jit(solution)/shard_map/pallas_call | solution.py:45
  127.1 14.2 %all_to_all.21.parts = f32[8,10,2,128]{3,2,1,0:T(2,128)S(1)} all-to-all(f32[8,10,2,128]{3,2,1,0:T(2,128)} %get-tuple-element.146), channel_id=1, replica_groups=mesh['x'=4,'z'=8,'y'=4,'core'=2] {'z'}, dimensions={0} | all-to-all | bytes 163840 | tf_op jit(solution)/shard_map/all_to_all | solution.py:412
  141.6 1.7 collective-permute-start.16
  143.3 2.4 collective-permute-start.15
  145.7 1.9 collective-permute-start.14
  147.9 1.6 collective-permute-start.12
  149.8 6.8 %all-to-all-start.2 = ((f32[16,2,64,256]{3,2,1,0:T(8,128)}), f32[16,2,64,256]{3,2,1,0:T(8,128)}, u32[]{:S(2)}, u32[]{:S(2)}) async-start(f32[16,2,64,256]{3,2,1,0:T(8,128)} %bitcast.17), calls=%async_computation.2 | async-start | bytes 4194304 | tf_op jit(solution)/shard_map/all_to_all | solution.py:412
  156.7 1.7 collective-permute-start.21
  160.7 1.9 collective-permute-start.20
  163.9 2.5 collective-permute-start.18
  166.4 38.1 %collective-permute-done.21.refs_1_ = f32[16,2,64,256]{3,2,1,0:T(8,128)} collective-permute-done((f32[16,2,64,256]{3,2,1,0:T(8,128)S(1)}, f32[16,2,64,256]{3,2,1,0:T(8,128)}, u32[]{:S(2)}, u32[]{:S(2)}) %collective-permute-start.21) | collective-permute-done | bytes 2097184 | tf_op jit(solution)/shard_map/ppermute | solution.py:408
  204.5 1.3 slice.80
  206.7 1.9 collective-permute-start.23
  210.6 21.1 %collective-permute-done.23.refs_3_ = f32[8,2,64,256]{3,2,1,0:T(8,128)S(1)} collective-permute-done((f32[8,2,64,256]{3,2,1,0:T(8,128)S(1)}, f32[8,2,64,256]{3,2,1,0:T(8,128)S(1)}, u32[]{:S(2)}, u32[]{:S(2)}) %collective-permute-start.23) | collective-permute-done | bytes 1048608 | tf_op jit(solution)/shard_map/ppermute | solution.py:408
  231.7 4.8 %collective-permute-done.24.refs_4_ = f32[8,2,64,256]{3,2,1,0:T(8,128)S(1)} collective-permute-done((f32[8,2,64,256]{3,2,1,0:T(8,128)S(1)}, f32[8,2,64,256]{3,2,1,0:T(8,128)S(1)}, u32[]{:S(2)}, u32[]{:S(2)}) %collective-permute-start.24) | collective-permute-done | bytes 1048608 | tf_op jit(solution)/shard_map/ppermute | solution.py:408
  236.5 2.6 %collective-permute-done.29.refs_9_ = f32[8,2,64,256]{3,2,1,0:T(8,128)S(1)} collective-permute-done((f32[8,2,64,256]{3,2,1,0:T(8,128)S(1)}, f32[8,2,64,256]{3,2,1,0:T(8,128)S(1)}, u32[]{:S(2)}, u32[]{:S(2)}) %collective-permute-start.29) | collective-permute-done | bytes 1048608 | tf_op jit(solution)/shard_map/ppermute | solution.py:459
  239.1 16.9 %shard_map.74 = f32[16,2,64,256]{3,2,1,0:T(8,128)} custom-call(s32[4]{0:T(128)S(1)} %copy-done.12, f32[136,128]{1,0:T(8,128)S(1)} %get-tuple-element.149.g0, f32[136,128]{1,0:T(8,128)S(1)} %collective-permute-done.18.g1, f32[136,128]{1,0:T(8,128)S(1)} %collective-permute-done.19.g2, f32[136,128]{1,0:T(8,128)S(1)} %collective-permute-done.20.g3, ...), custom_call_target="tpu_custom_call" | custom-call | flops 134217728 | bytes 16777216 | tf_op jit(solution)/shard_map/pallas_call | solution.py:45
  256.0 3.1 %copy.14 = f32[16,2,64,256]{3,2,1,0:T(8,128)} copy(f32[16,2,64,256]{3,2,1,0:T(8,128)} %all-to-all-done.2) | data formatting | bytes 4194304
  (94 shorter events, 20.9 us)
Async XLA Ops:
  16.6 6.0 %collective-permute-start.10 = (f32[2,2,8,256]{3,2,1,0:T(8,128)S(1)}, f32[2,2,8,256]{3,2,1,0:T(8,128)S(1)}, u32[]{:S(2)}, u32[]{:S(2)}) collective-permute-start(f32[2,2,8,256]{3,2,1,0:T(8,128)S(1)} %get-tuple-element.193), channel_id=1, source_target_pairs={{64,0},{128,64},{192,128},{65,1},{129,65},{193,129},{66,2},{130,66... | collective-permute-start | bytes 98312 | tf_op jit(solution)/shard_map/ppermute | solution.py:483
  17.9 6.3 %collective-permute-start.9 = (f32[2,2,8,256]{3,2,1,0:T(8,128)S(1)}, f32[2,2,8,256]{3,2,1,0:T(8,128)S(1)}, u32[]{:S(2)}, u32[]{:S(2)}) collective-permute-start(f32[2,2,8,256]{3,2,1,0:T(8,128)S(1)} %get-tuple-element.194), channel_id=1, source_target_pairs={{0,64},{64,128},{128,192},{1,65},{65,129},{129,193},{2,66},{66,130... | collective-permute-start | bytes 98312 | tf_op jit(solution)/shard_map/ppermute | solution.py:482
  25.4 79.8 %all-to-all-start.1 = ((f32[8,24,8,256]{3,2,1,0:T(8,128)}), f32[8,24,8,256]{3,2,1,0:T(8,128)}, u32[]{:S(2)}, u32[]{:S(2)}) async-start(f32[8,24,8,256]{3,2,1,0:T(8,128)} %copy-done.2), calls=%async_computation.1 | async-start | bytes 3145728 | tf_op jit(solution)/shard_map/all_to_all | solution.py:412
  31.0 11.9 %collective-permute-start.6 = (f32[2,2,64,256]{3,2,1,0:T(8,128)S(1)}, f32[2,2,64,256]{3,2,1,0:T(8,128)S(1)}, u32[]{:S(2)}, u32[]{:S(2)}) collective-permute-start(f32[2,2,64,256]{3,2,1,0:T(8,128)S(1)} %get-tuple-element.185), channel_id=1, source_target_pairs={{56,0},{0,8},{8,16},{16,24},{24,32},{32,40},{40,48},{48,56},{57,1}... | collective-permute-start | bytes 786440 | tf_op jit(solution)/shard_map/ppermute | solution.py:408
  32.1 18.0 %collective-permute-start.5 = (f32[2,2,64,256]{3,2,1,0:T(8,128)S(1)}, f32[2,2,64,256]{3,2,1,0:T(8,128)S(1)}, u32[]{:S(2)}, u32[]{:S(2)}) collective-permute-start(f32[2,2,64,256]{3,2,1,0:T(8,128)S(1)} %get-tuple-element.186), channel_id=1, source_target_pairs={{48,0},{56,8},{0,16},{8,24},{16,32},{24,40},{32,48},{40,56},{49,1}... | collective-permute-start | bytes 786440 | tf_op jit(solution)/shard_map/ppermute | solution.py:408
  33.4 49.2 %collective-permute-start.4 = (f32[2,2,64,256]{3,2,1,0:T(8,128)}, f32[2,2,64,256]{3,2,1,0:T(8,128)S(1)}, u32[]{:S(2)}, u32[]{:S(2)}) collective-permute-start(f32[2,2,64,256]{3,2,1,0:T(8,128)} %get-tuple-element.187), channel_id=1, source_target_pairs={{40,0},{48,8},{56,16},{0,24},{8,32},{16,40},{24,48},{32,56},{41,1}... | collective-permute-start | bytes 786440 | tf_op jit(solution)/shard_map/ppermute | solution.py:408
  38.0 44.5 %collective-permute-start.3 = (f32[2,2,64,256]{3,2,1,0:T(8,128)}, f32[2,2,64,256]{3,2,1,0:T(8,128)S(1)}, u32[]{:S(2)}, u32[]{:S(2)}) collective-permute-start(f32[2,2,64,256]{3,2,1,0:T(8,128)} %get-tuple-element.188), channel_id=1, source_target_pairs={{32,0},{40,8},{48,16},{56,24},{0,32},{8,40},{16,48},{24,56},{33,1}... | collective-permute-start | bytes 786440 | tf_op jit(solution)/shard_map/ppermute | solution.py:408
  38.6 44.0 %collective-permute-start.2 = (f32[2,2,64,256]{3,2,1,0:T(8,128)}, f32[2,2,64,256]{3,2,1,0:T(8,128)S(1)}, u32[]{:S(2)}, u32[]{:S(2)}) collective-permute-start(f32[2,2,64,256]{3,2,1,0:T(8,128)} %get-tuple-element.189), channel_id=1, source_target_pairs={{24,0},{32,8},{40,16},{48,24},{56,32},{0,40},{8,48},{16,56},{25,1}... | collective-permute-start | bytes 786440 | tf_op jit(solution)/shard_map/ppermute | solution.py:408
  42.9 39.7 %collective-permute-start.1 = (f32[2,2,64,256]{3,2,1,0:T(8,128)}, f32[2,2,64,256]{3,2,1,0:T(8,128)S(1)}, u32[]{:S(2)}, u32[]{:S(2)}) collective-permute-start(f32[2,2,64,256]{3,2,1,0:T(8,128)} %get-tuple-element.190), channel_id=1, source_target_pairs={{16,0},{24,8},{32,16},{40,24},{48,32},{56,40},{0,48},{8,56},{17,1}... | collective-permute-start | bytes 786440 | tf_op jit(solution)/shard_map/ppermute | solution.py:408
  50.1 35.2 %collective-permute-start = (f32[2,2,64,256]{3,2,1,0:T(8,128)}, f32[2,2,64,256]{3,2,1,0:T(8,128)S(1)}, u32[]{:S(2)}, u32[]{:S(2)}) collective-permute-start(f32[2,2,64,256]{3,2,1,0:T(8,128)} %get-tuple-element.191), channel_id=1, source_target_pairs={{8,0},{16,8},{24,16},{32,24},{40,32},{48,40},{56,48},{0,56},{9,1},... | collective-permute-start | bytes 786440 | tf_op jit(solution)/shard_map/ppermute | solution.py:408
  86.4 14.7 %collective-permute-start.7 = (f32[2,4,64,256]{3,2,1,0:T(8,128)S(1)}, f32[2,4,64,256]{3,2,1,0:T(8,128)S(1)}, u32[]{:S(2)}, u32[]{:S(2)}) collective-permute-start(f32[2,4,64,256]{3,2,1,0:T(8,128)S(1)} %get-tuple-element.143), channel_id=1, source_target_pairs={{0,64},{64,128},{128,192},{1,65},{65,129},{129,193},{2,66},{66,130... | collective-permute-start | bytes 1572872 | tf_op jit(solution)/shard_map/ppermute | solution.py:545
  90.6 14.6 %collective-permute-start.8 = (f32[2,4,64,256]{3,2,1,0:T(8,128)S(1)}, f32[2,4,64,256]{3,2,1,0:T(8,128)S(1)}, u32[]{:S(2)}, u32[]{:S(2)}) collective-permute-start(f32[2,4,64,256]{3,2,1,0:T(8,128)S(1)} %get-tuple-element.144), channel_id=1, source_target_pairs={{64,0},{128,64},{192,128},{65,1},{129,65},{193,129},{66,2},{130,66... | collective-permute-start | bytes 1572872 | tf_op jit(solution)/shard_map/ppermute | solution.py:545
  141.3 6.6 %collective-permute-start.17 = (f32[10,16,128]{2,1,0:T(8,128)S(1)}, f32[10,16,128]{2,1,0:T(8,128)S(1)}, u32[]{:S(2)}, u32[]{:S(2)}) collective-permute-start(f32[10,16,128]{2,1,0:T(8,128)S(1)} %shard_map.72.refs_0_), channel_id=1, source_target_pairs={{7,0},{6,1},{1,2},{0,3},{3,4},{2,5},{5,6},{4,7},{15,8},{14,9},{9,1... | collective-permute-start | bytes 245768 | tf_op jit(solution)/shard_map/ppermute | solution.py:451
  141.6 7.9 %collective-permute-start.16 = (f32[10,16,128]{2,1,0:T(8,128)S(1)}, f32[10,16,128]{2,1,0:T(8,128)S(1)}, u32[]{:S(2)}, u32[]{:S(2)}) collective-permute-start(f32[10,16,128]{2,1,0:T(8,128)S(1)} %shard_map.72.refs_0_), channel_id=1, source_target_pairs={{6,0},{7,1},{0,2},{1,3},{2,4},{3,5},{4,6},{5,7},{14,8},{15,9},{8,1... | collective-permute-start | bytes 245768 | tf_op jit(solution)/shard_map/ppermute | solution.py:451
  143.3 13.3 %collective-permute-start.15 = (f32[10,16,128]{2,1,0:T(8,128)S(1)}, f32[10,16,128]{2,1,0:T(8,128)S(1)}, u32[]{:S(2)}, u32[]{:S(2)}) collective-permute-start(f32[10,16,128]{2,1,0:T(8,128)S(1)} %shard_map.72.refs_0_), channel_id=1, source_target_pairs={{5,0},{4,1},{7,2},{6,3},{1,4},{0,5},{3,6},{2,7},{13,8},{12,9},{15,... | collective-permute-start | bytes 245768 | tf_op jit(solution)/shard_map/ppermute | solution.py:451
  145.7 12.6 %collective-permute-start.14 = (f32[10,16,128]{2,1,0:T(8,128)S(1)}, f32[10,16,128]{2,1,0:T(8,128)S(1)}, u32[]{:S(2)}, u32[]{:S(2)}) collective-permute-start(f32[10,16,128]{2,1,0:T(8,128)S(1)} %shard_map.72.refs_0_), channel_id=1, source_target_pairs={{4,0},{5,1},{6,2},{7,3},{0,4},{1,5},{2,6},{3,7},{12,8},{13,9},{14,... | collective-permute-start | bytes 245768 | tf_op jit(solution)/shard_map/ppermute | solution.py:451
  147.6 11.1 %collective-permute-start.13 = (f32[10,16,128]{2,1,0:T(8,128)S(1)}, f32[10,16,128]{2,1,0:T(8,128)S(1)}, u32[]{:S(2)}, u32[]{:S(2)}) collective-permute-start(f32[10,16,128]{2,1,0:T(8,128)S(1)} %shard_map.72.refs_0_), channel_id=1, source_target_pairs={{3,0},{2,1},{5,2},{4,3},{7,4},{6,5},{1,6},{0,7},{11,8},{10,9},{13,... | collective-permute-start | bytes 245768 | tf_op jit(solution)/shard_map/ppermute | solution.py:451
  147.9 10.9 %collective-permute-start.12 = (f32[10,16,128]{2,1,0:T(8,128)S(1)}, f32[10,16,128]{2,1,0:T(8,128)S(1)}, u32[]{:S(2)}, u32[]{:S(2)}) collective-permute-start(f32[10,16,128]{2,1,0:T(8,128)S(1)} %shard_map.72.refs_0_), channel_id=1, source_target_pairs={{2,0},{3,1},{4,2},{5,3},{6,4},{7,5},{0,6},{1,7},{10,8},{11,9},{12,... | collective-permute-start | bytes 245768 | tf_op jit(solution)/shard_map/ppermute | solution.py:451
  149.5 9.3 %collective-permute-start.11 = (f32[10,16,128]{2,1,0:T(8,128)S(1)}, f32[10,16,128]{2,1,0:T(8,128)S(1)}, u32[]{:S(2)}, u32[]{:S(2)}) collective-permute-start(f32[10,16,128]{2,1,0:T(8,128)S(1)} %shard_map.72.refs_0_), channel_id=1, source_target_pairs={{1,0},{0,1},{3,2},{2,3},{5,4},{4,5},{7,6},{6,7},{9,8},{8,9},{11,10... | collective-permute-start | bytes 245768 | tf_op jit(solution)/shard_map/ppermute | solution.py:451
  149.8 106.2 %all-to-all-start.2 = ((f32[16,2,64,256]{3,2,1,0:T(8,128)}), f32[16,2,64,256]{3,2,1,0:T(8,128)}, u32[]{:S(2)}, u32[]{:S(2)}) async-start(f32[16,2,64,256]{3,2,1,0:T(8,128)} %bitcast.17), calls=%async_computation.2 | async-start | bytes 4194304 | tf_op jit(solution)/shard_map/all_to_all | solution.py:412
  156.7 47.8 %collective-permute-start.21 = (f32[16,2,64,256]{3,2,1,0:T(8,128)S(1)}, f32[16,2,64,256]{3,2,1,0:T(8,128)}, u32[]{:S(2)}, u32[]{:S(2)}) collective-permute-start(f32[16,2,64,256]{3,2,1,0:T(8,128)S(1)} %copy-done.1), channel_id=1, source_target_pairs={{2,0},{4,2},{6,4},{0,6},{3,1},{5,3},{7,5},{1,7},{10,8},{12,10},{14... | collective-permute-start | bytes 6291464 | tf_op jit(solution)/shard_map/ppermute | solution.py:408
  158.4 48.3 %collective-permute-start.22 = (f32[16,2,64,256]{3,2,1,0:T(8,128)S(1)}, f32[16,2,64,256]{3,2,1,0:T(8,128)}, u32[]{:S(2)}, u32[]{:S(2)}) collective-permute-start(f32[16,2,64,256]{3,2,1,0:T(8,128)S(1)} %copy-done.1), channel_id=1, source_target_pairs={{6,0},{0,2},{2,4},{4,6},{7,1},{1,3},{3,5},{5,7},{14,8},{8,10},{10,... | collective-permute-start | bytes 6291464 | tf_op jit(solution)/shard_map/ppermute | solution.py:408
  160.7 49.2 %collective-permute-start.20 = (f32[136,128]{1,0:T(8,128)S(1)}, f32[136,128]{1,0:T(8,128)S(1)}, u32[]{:S(2)}, u32[]{:S(2)}) collective-permute-start(f32[136,128]{1,0:T(8,128)S(1)} %get-tuple-element.149.g0), channel_id=1, source_target_pairs={{192,0},{0,64},{64,128},{128,192},{193,1},{1,65},{65,129},{129,193... | collective-permute-start | bytes 208904 | tf_op jit(solution)/shard_map/ppermute | solution.py:408
  162.6 47.5 %collective-permute-start.19 = (f32[136,128]{1,0:T(8,128)S(1)}, f32[136,128]{1,0:T(8,128)S(1)}, u32[]{:S(2)}, u32[]{:S(2)}) collective-permute-start(f32[136,128]{1,0:T(8,128)S(1)} %get-tuple-element.149.g0), channel_id=1, source_target_pairs={{128,0},{192,64},{0,128},{64,192},{129,1},{193,65},{1,129},{65,193... | collective-permute-start | bytes 208904 | tf_op jit(solution)/shard_map/ppermute | solution.py:408
  163.9 46.4 %collective-permute-start.18 = (f32[136,128]{1,0:T(8,128)S(1)}, f32[136,128]{1,0:T(8,128)S(1)}, u32[]{:S(2)}, u32[]{:S(2)}) collective-permute-start(f32[136,128]{1,0:T(8,128)S(1)} %get-tuple-element.149.g0), channel_id=1, source_target_pairs={{64,0},{128,64},{192,128},{0,192},{65,1},{129,65},{193,129},{1,193... | collective-permute-start | bytes 208904 | tf_op jit(solution)/shard_map/ppermute | solution.py:408
  204.5 32.0 %collective-permute-start.25 = (f32[16,2,64,256]{3,2,1,0:T(8,128)S(1)}, f32[16,2,64,256]{3,2,1,0:T(8,128)S(1)}, u32[]{:S(2)}, u32[]{:S(2)}) collective-permute-start(f32[16,2,64,256]{3,2,1,0:T(8,128)S(1)} %copy-done.1), channel_id=1, source_target_pairs={{0,1},{1,0},{2,3},{3,2},{4,5},{5,4},{6,7},{7,6},{8,9},{9,8},{10,11... | collective-permute-start | bytes 6291464 | tf_op jit(solution)/shard_map/ppermute | solution.py:459
  206.7 25.0 %collective-permute-start.23 = (f32[8,2,64,256]{3,2,1,0:T(8,128)S(1)}, f32[8,2,64,256]{3,2,1,0:T(8,128)S(1)}, u32[]{:S(2)}, u32[]{:S(2)}) collective-permute-start(f32[8,2,64,256]{3,2,1,0:T(8,128)S(1)} %slice.80), channel_id=1, source_target_pairs={{2,0},{4,2},{6,4},{0,6},{3,1},{5,3},{7,5},{1,7},{10,8},{12,10},{14... | collective-permute-start | bytes 3145736 | tf_op jit(solution)/shard_map/ppermute | solution.py:408
  209.9 26.6 %collective-permute-start.24 = (f32[8,2,64,256]{3,2,1,0:T(8,128)S(1)}, f32[8,2,64,256]{3,2,1,0:T(8,128)S(1)}, u32[]{:S(2)}, u32[]{:S(2)}) collective-permute-start(f32[8,2,64,256]{3,2,1,0:T(8,128)S(1)} %slice.81), channel_id=1, source_target_pairs={{6,0},{0,2},{2,4},{4,6},{7,1},{1,3},{3,5},{5,7},{14,8},{8,10},{10,... | collective-permute-start | bytes 3145736 | tf_op jit(solution)/shard_map/ppermute | solution.py:408
  210.1 26.4 %collective-permute-start.26 = (f32[16,2,64,256]{3,2,1,0:T(8,128)}, f32[16,2,64,256]{3,2,1,0:T(8,128)S(1)}, u32[]{:S(2)}, u32[]{:S(2)}) collective-permute-start(f32[16,2,64,256]{3,2,1,0:T(8,128)} %collective-permute-done.21.refs_1_), channel_id=1, source_target_pairs={{0,1},{1,0},{2,3},{3,2},{4,5},{5,4},{6,7},{7,6},{8,9},{9,8},{10,11... | collective-permute-start | bytes 6291464 | tf_op jit(solution)/shard_map/ppermute | solution.py:459
  210.3 28.8 %collective-permute-start.27 = (f32[16,2,64,256]{3,2,1,0:T(8,128)}, f32[16,2,64,256]{3,2,1,0:T(8,128)S(1)}, u32[]{:S(2)}, u32[]{:S(2)}) collective-permute-start(f32[16,2,64,256]{3,2,1,0:T(8,128)} %collective-permute-done.22.refs_2_), channel_id=1, source_target_pairs={{0,1},{1,0},{2,3},{3,2},{4,5},{5,4},{6,7},{7,6},{8,9},{9,8},{10,11... | collective-permute-start | bytes 6291464 | tf_op jit(solution)/shard_map/ppermute | solution.py:459
  231.7 4.8 %collective-permute-start.28 = (f32[8,2,64,256]{3,2,1,0:T(8,128)S(1)}, f32[8,2,64,256]{3,2,1,0:T(8,128)S(1)}, u32[]{:S(2)}, u32[]{:S(2)}) collective-permute-start(f32[8,2,64,256]{3,2,1,0:T(8,128)S(1)} %collective-permute-done.23.refs_3_), channel_id=1, source_target_pairs={{0,1},{1,0},{2,3},{3,2},{4,5},{5,4},{6,7},{7,6},{8,9},{9,8},{10,11... | collective-permute-start | bytes 3145736 | tf_op jit(solution)/shard_map/ppermute | solution.py:459
  236.5 2.7 %collective-permute-start.29 = (f32[8,2,64,256]{3,2,1,0:T(8,128)S(1)}, f32[8,2,64,256]{3,2,1,0:T(8,128)S(1)}, u32[]{:S(2)}, u32[]{:S(2)}) collective-permute-start(f32[8,2,64,256]{3,2,1,0:T(8,128)S(1)} %collective-permute-done.24.refs_4_), channel_id=1, source_target_pairs={{0,1},{1,0},{2,3},{3,2},{4,5},{5,4},{6,7},{7,6},{8,9},{9,8},{10,11... | collective-permute-start | bytes 3145736 | tf_op jit(solution)/shard_map/ppermute | solution.py:459
  (18 other events, 410.1 us)
